TPU v7x, 512 devices: a whole 4x8x8 slice. The times are simulated.
512 devices in a mesh: ens: 4 (over y_hi), lat: 2 (over core), lon: 64 (over y_lo, z, x).
Axes of the slice: x: 4, y: 8 (y_hi: 4, y_lo: 2; y = y_hi * 2 + y_lo), z: 8, core: 2. Of those that a mesh axis runs over, the one named last changes fastest.
Arguments:
- fields: bfloat16 [8, 36, 1536, 384], P('ens', 'lat', 'lon'), parts along dimension 0, may hold values from -6 to 6
- region_ids: int32 [2, 36, 1536], P(None, 'lat', 'lon'), may hold values from 0 to 3
- bias_index: int32 [144, 144], replicated, may hold values from 0 to 3311
- earth_bias: bfloat16 [6, 3312, 12], P('lat'), may hold values from -70 to 170
- w_qkv: bfloat16 [384, 1152], replicated, may hold values from -0.3125 to 0.3125
- w_proj: bfloat16 [384, 384], replicated, may hold values from -0.3125 to 0.3125
- w_fc1: bfloat16 [384, 1536], replicated, may hold values from -0.3125 to 0.3125
- w_fc2: bfloat16 [1536, 384], replicated, may hold values from -0.15625 to 0.15625
Outputs:
- result: bfloat16 [8, 36, 1536, 384], P('ens', 'lat', 'lon'), parts along dimension 0
There are 4 independent parts, one for each index of `ens`. A program takes and returns all parts, laid end to end along the dimension named above; an argument that names none is the same for every part. Nothing has to cross between parts.
All inputs are finite; a program needn't handle non-finite values.
Results may differ from a plain program's by a relative error of at most 0.009.
Values may be sent and summed in bfloat16 or wider, within the bound.
No kernel may reach another device: no remote copies, remote signals or barrier semaphores. Data moves between devices by JAX's collectives and lax.ppermute only.
A program may use at most 128 MiB of HBM per device.

v0:
```python
import jax
import jax.numpy as jnp
from jax import lax
from jax.sharding import PartitionSpec as P

WZ = 2
WLAT = 6
WLON = 12


EPS_NORM = 1e-05


def from_behind(value, axis, steps):
    count = lax.axis_size(axis)
    pairs = [(source, (source + steps) % count) for source in range(count)]
    return lax.ppermute(value, axis, pairs)


def layer_norm(tokens_in):
    widened = tokens_in.astype(jnp.float32)
    average = jnp.mean(widened, axis=-1, keepdims=True)
    centred = widened - average
    spread = jnp.mean(centred * centred, axis=-1, keepdims=True)
    return (centred * lax.rsqrt(spread + EPS_NORM)).astype(jnp.bfloat16)


def bias_scores(earth_bias, bias_index):
    bands, positions, head_count = earth_bias.shape
    window_tokens = bias_index.shape[0]
    flat_table = earth_bias.transpose(0, 2, 1).reshape(bands * head_count, positions)
    picked = jnp.take(flat_table, bias_index.reshape(-1), axis=1)
    return picked.astype(jnp.float32).reshape(bands, head_count, window_tokens, window_tokens)


def attend(normed, region_block, bias_table, w_qkv, w_proj):
    levels, lat_rows, lon_cols, feature_width = normed.shape
    lat_wins = lat_rows // WLAT
    lon_wins = lon_cols // WLON
    window_tokens = levels * WLAT * WLON
    head_count = bias_table.shape[1]
    head_dim = feature_width // head_count
    windowed = normed.reshape(levels, lat_wins, WLAT, lon_wins, WLON, feature_width)
    windowed = windowed.transpose(1, 3, 0, 2, 4, 5).reshape(-1, feature_width)
    packed = jnp.dot(windowed, w_qkv, preferred_element_type=jnp.float32).astype(jnp.bfloat16)
    packed = packed.reshape(lat_wins, lon_wins, window_tokens, 3, head_count, head_dim)
    queries = packed[:, :, :, 0]
    key_rows = packed[:, :, :, 1]
    value_rows = packed[:, :, :, 2]
    regions = region_block.reshape(levels, lat_wins, WLAT, lon_wins, WLON)
    regions = regions.transpose(1, 3, 0, 2, 4).reshape(lat_wins, lon_wins, window_tokens)
    scores = jnp.einsum("abihd,abjhd->abhij", queries, key_rows, preferred_element_type=jnp.float32)
    scores = scores * head_dim ** (-0.5) + bias_table[:, None]
    allowed = regions[:, :, :, None] == regions[:, :, None, :]
    scores = jnp.where(allowed[:, :, None], scores, -jnp.inf)
    maxima = jnp.max(scores, axis=-1, keepdims=True)
    exponent = jnp.exp(scores - maxima)
    attn_weights = (exponent / jnp.sum(exponent, axis=-1, keepdims=True)).astype(jnp.bfloat16)
    context = jnp.einsum(
        "abhij,abjhd->abihd", attn_weights, value_rows, preferred_element_type=jnp.float32
    )
    context = context.astype(jnp.bfloat16).reshape(-1, feature_width)
    projected = jnp.dot(context, w_proj, preferred_element_type=jnp.float32).astype(jnp.bfloat16)
    projected = projected.reshape(lat_wins, lon_wins, levels, WLAT, WLON, feature_width)
    return projected.transpose(2, 0, 3, 1, 4, 5).reshape(levels, lat_rows, lon_cols, feature_width)


def feed_forward(residual, w_fc1, w_fc2):
    feature_width = residual.shape[-1]
    normed = layer_norm(residual).reshape(-1, feature_width)
    hidden = jax.nn.gelu(
        jnp.dot(normed, w_fc1, preferred_element_type=jnp.float32), approximate=False
    )
    hidden = hidden.astype(jnp.bfloat16)
    summed = residual.reshape(-1, feature_width).astype(jnp.float32) + jnp.dot(
        hidden, w_fc2, preferred_element_type=jnp.float32
    )
    return summed.astype(jnp.bfloat16).reshape(residual.shape)


def forward_shift(source):
    half_lev = WZ // 2
    half_lat = WLAT // 2
    half_lon = WLON // 2
    arrived = from_behind(source[:, :, :half_lon], "lon", -1)
    along_lon = jnp.concatenate([source[:, :, half_lon:], arrived], axis=2)
    rows_sent = from_behind(along_lon[:, :half_lat], "lat", -1)
    along_lat = jnp.concatenate([along_lon[:, half_lat:], rows_sent], axis=1)
    return jnp.roll(along_lat, -half_lev, axis=0)


def backward_shift(shifted_result):
    half_lev = WZ // 2
    half_lat = WLAT // 2
    half_lon = WLON // 2
    rolled = jnp.roll(shifted_result, half_lev, axis=0)
    rows_back = from_behind(rolled[:, -half_lat:], "lat", 1)
    along_lat = jnp.concatenate([rows_back, rolled[:, :-half_lat]], axis=1)
    cols_back = from_behind(along_lat[:, :, -half_lon:], "lon", 1)
    return jnp.concatenate([cols_back, along_lat[:, :, :-half_lon]], axis=2)


def local(fields, region_ids, bias_index, earth_bias, w_qkv, w_proj, w_fc1, w_fc2):
    bias_table = bias_scores(earth_bias, bias_index)
    source = layer_norm(fields)
    shifted = forward_shift(source)
    attn_out = attend(shifted, region_ids, bias_table, w_qkv, w_proj)
    returned = backward_shift(attn_out)
    residual = (fields.astype(jnp.float32) + returned.astype(jnp.float32)).astype(jnp.bfloat16)
    return feed_forward(residual, w_fc1, w_fc2)


def solution(mesh):
    return jax.shard_map(
        local,
        mesh=mesh,
        in_specs=(
            P("ens", "lat", "lon", None),
            P(None, "lat", "lon"),
            P(),
            P("lat", None, None),
            P(),
            P(),
            P(),
            P(),
        ),
        out_specs=P("ens", "lat", "lon", None),
        check_vma=False,
    )
```

profile of v0, /device:TPU:1, one launch (start us, length us, event | category | flops | bytes accessed | tf_op | source)
XLA Modules:
  0.0 166.0 jit_solution(16476902176667628981)
XLA Ops:
  0.0 1.4 convert_reduce_fusion
  1.4 1.5 fusion.26
  2.9 1.4 fusion.27
  4.3 0.7 slice.75
  5.0 14.7 %collective-permute-start = (bf16[2,18,6,384]{3,2,1,0:T(8,128)(2,1)}, bf16[2,18,6,384]{3,2,1,0:T(8,128)(2,1)}, u32[]{:S(2)}, u32[]{:S(2)}) collective-permute-start(bf16[2,18,6,384]{3,2,1,0:T(8,128)(2,1)} %slice.75), channel_id=1, source_target_pairs={{0,63},{1,0},{2,1},{3,2},{4,3},{5,4},{6,5},{7,6},{8,7},{9,8},{10,9... | collective-permute-start | bytes 497672 | tf_op jit(solution)/shard_map/ppermute | solution.py:17
  19.7 1.0 compare_and_fusion
  20.6 1.1 reshape.114
  22.0 0.8 reshape.112
  23.2 1.1 reshape.113
  24.7 42.0 %gather_fusion = bf16[20736,36]{1,0:T(8,128)(2,1)} fusion(bf16[36,3312]{0,1:T(8,128)(2,1)S(1)} %copy.25, s32[21504]{0:T(1024)S(1)} %pad_clamp_fusion), kind=kCustom, calls=%fused_computation | custom fusion | bytes 3068928 | tf_op jit(solution)/shard_map/jit(_take)/gather | solution.py:32
  66.7 5.1 %copy.26 = bf16[36,20736]{1,0:T(8,128)(2,1)S(1)} copy(bf16[36,20736]{0,1:T(8,128)(2,1)} %bitcast.53) | data formatting | bytes 2985984 | tf_op jit(solution)/shard_map/jit(_take)/gather | solution.py:32
  71.9 6.6 %gather.7 = bf16[3,12,144,144]{3,2,1,0:T(8,128)(2,1)} reshape(bf16[36,20736]{1,0:T(8,128)(2,1)S(1)} %copy.26) | data formatting | bytes 2985984 | tf_op jit(solution)/shard_map/jit(_take)/gather | solution.py:32
  78.5 4.4 %select_convert_fusion = f32[3,12,144,144]{3,2,1,0:T(8,128)} fusion(bf16[3,12,144,144]{3,2,1,0:T(8,128)(2,1)} %gather.7, pred[144,144]{1,0:T(8,128)(4,1)S(1)} %compare_and_fusion), kind=kLoop, calls=%fused_computation.32 | loop fusion | flops 1492992 | bytes 4499712 | tf_op jit(solution)/shard_map/convert_element_type | solution.py:33
  82.9 6.6 %copy.27 = f32[3,12,144,144]{2,3,1,0:T(8,128)} copy(f32[3,12,144,144]{3,2,1,0:T(8,128)} %select_convert_fusion) | data formatting | bytes 5971968 | tf_op jit(solution)/shard_map/convert_element_type | solution.py:33
  89.5 0.9 broadcast_compare_fusion
  90.4 0.8 pad_maximum_fusion.3
  91.2 2.9 %collective-permute-start.1 = (bf16[2,3,24,384]{3,2,1,0:T(8,128)(2,1)S(1)}, bf16[2,3,24,384]{3,2,1,0:T(8,128)(2,1)S(1)}, u32[]{:S(2)}, u32[]{:S(2)}) collective-permute-start(bf16[2,3,24,384]{3,2,1,0:T(8,128)(2,1)S(1)} %pad_maximum_fusion.3), channel_id=1, source_target_pairs={{0,64},{64,0},{1,65},{65,1},{2,66},{66,2},{3,67},{67,3},{4,68},{68... | collective-permute-start | bytes 331784 | tf_op jit(solution)/shard_map/ppermute | solution.py:17
  94.1 1.0 fusion.32
  96.1 3.7 %convolution_convert_fusion = bf16[864,1152]{1,0:T(8,128)(2,1)} fusion(bf16[864,384]{1,0:T(8,128)(2,1)S(1)} %reshape.110, bf16[384,1152]{1,0:T(8,128)(2,1)} %param.12), kind=kOutput, calls=%fused_computation.31 | convolution fusion | flops 765407232 | bytes 3538944 | tf_op jit(solution)/shard_map/dot_general | solution.py:45
  99.8 2.9 %copy.20 = bf16[864,1152]{0,1:T(8,128)(2,1)S(1)} copy(bf16[864,1152]{1,0:T(8,128)(2,1)} %convolution_convert_fusion) | data formatting | bytes 3981312 | tf_op jit(solution)/shard_map/convert_element_type | solution.py:45
  102.6 4.1 %reshape.111 = bf16[3,2,144,3,12,32]{2,1,0,5,4,3:T(2,128)(2,1)} reshape(bf16[864,1152]{0,1:T(8,128)(2,1)S(1)} %copy.20) | data formatting | bytes 3981312 | tf_op jit(solution)/shard_map/reshape | solution.py:46
  106.7 5.3 %fusion.68 = (bf16[3,2,144,1,12,32]{2,1,0,5,4,3:T(2,128)(2,1)S(1)}, bf16[3,2,144,1,12,32]{2,1,0,5,4,3:T(2,128)(2,1)S(1)}, bf16[3,2,144,1,12,32]{2,1,0,5,4,3:T(2,128)(2,1)}) fusion(bf16[3,2,144,3,12,32]{2,1,0,5,4,3:T(2,128)(2,1)} %reshape.111), kind=kLoop, calls=%fused_computation.111 | loop fusion | bytes 3981312 | tf_op jit(solution)/shard_map/slice | solution.py:49
  112.0 11.8 %fusion.70 = (f32[3,2,12,144]{3,2,1,0:T(8,128)}, f32[3,2,12,144,144]{3,4,2,1,0:T(8,128)}) fusion(f32[3,12,144,144]{2,3,1,0:T(8,128)} %copy.27, pred[3,2,144,144]{2,3,1,0:T(8,128)(4,1)} %broadcast_compare_fusion, bf16[3,2,144,1,12,32]{2,1,0,5,4,3:T(2,128)(2,1)S(1)} %get-tuple-element.8, bf16[3,2,144,1,12,32]{2,1,0,5,4,3:T(2,128)(2,1)} %get-tuple-element.9), kind=kOutput, calls=%fused_computation.113 | convolution fusion | flops 103016592 | bytes 10450944 | tf_op jit(solution)/shard_map/sub | solution.py:57
  123.7 4.9 %fusion.22 = bf16[3,2,144,12,32]{2,4,3,1,0:T(8,128)(2,1)S(1)} fusion(f32[3,2,12,144,144]{3,4,2,1,0:T(8,128)} %get-tuple-element.13, f32[3,2,12,144]{3,2,1,0:T(8,128)} %get-tuple-element.12, bf16[3,2,144,1,12,32]{2,1,0,5,4,3:T(2,128)(2,1)S(1)} %get-tuple-element.7), kind=kOutput, calls=%fused_computation.39 | convolution fusion | flops 98869248 | bytes 7340544 | tf_op jit(solution)/shard_map/abhij,abjhd->abihd/dot_general | solution.py:59
  128.7 1.2 copy.29
  130.5 1.4 convolution_convert_fusion.1
  132.0 1.3 reshape.116
  133.8 2.1 %collective-permute-start.2 = (bf16[2,3,24,384]{3,2,1,0:T(8,128)(2,1)S(1)}, bf16[2,3,24,384]{3,2,1,0:T(8,128)(2,1)S(1)}, u32[]{:S(2)}, u32[]{:S(2)}) collective-permute-start(bf16[2,3,24,384]{3,2,1,0:T(8,128)(2,1)S(1)} %slice.85), channel_id=1, source_target_pairs={{0,64},{64,0},{1,65},{65,1},{2,66},{66,2},{3,67},{67,3},{4,68},{68... | collective-permute-start | bytes 331784 | tf_op jit(solution)/shard_map/ppermute | solution.py:17
  136.0 1.0 collective-permute-done.2
  137.0 2.1 %collective-permute-start.3 = (bf16[2,18,6,384]{3,2,1,0:T(8,128)(2,1)S(1)}, bf16[2,18,6,384]{3,2,1,0:T(8,128)(2,1)S(1)}, u32[]{:S(2)}, u32[]{:S(2)}) collective-permute-start(bf16[2,18,6,384]{3,2,1,0:T(8,128)(2,1)S(1)} %pad_maximum_fusion.2), channel_id=1, source_target_pairs={{0,1},{1,2},{2,3},{3,4},{4,5},{5,6},{6,7},{7,8},{8,9},{9,10},{10,1... | collective-permute-start | bytes 497672 | tf_op jit(solution)/shard_map/ppermute | solution.py:17
  139.2 10.7 %collective-permute-done.3 = bf16[2,18,6,384]{3,2,1,0:T(8,128)(2,1)S(1)} collective-permute-done((bf16[2,18,6,384]{3,2,1,0:T(8,128)(2,1)S(1)}, bf16[2,18,6,384]{3,2,1,0:T(8,128)(2,1)S(1)}, u32[]{:S(2)}, u32[]{:S(2)}) %collective-permute-start.3) | collective-permute-done | bytes 165920 | tf_op jit(solution)/shard_map/ppermute | solution.py:17
  151.1 14.9 %fusion.25 = bf16[864,384]{1,0:T(8,128)(2,1)} fusion(bf16[1536,384]{1,0:T(8,128)(2,1)S(1)} %copy-done, bf16[864,384]{1,0:T(8,128)(2,1)S(1)} %bitcast.57, bf16[384,1536]{1,0:T(8,128)(2,1)} %param.14, bf16[864,384]{1,0:T(8,128)(2,1)S(1)} %bitcast.54), kind=kOutput, calls=%fused_computation.42 | convolution fusion | flops 2125688832 | bytes 4349952 | tf_op jit(solution)/shard_map/dot_general | solution.py:75
  (37 shorter events, 4.3 us)
Async XLA Ops:
  0.0 151.1 %copy-start = (bf16[1536,384]{1,0:T(8,128)(2,1)S(1)}, bf16[1536,384]{1,0:T(8,128)(2,1)}, u32[]{:S(2)}) copy-start(bf16[1536,384]{1,0:T(8,128)(2,1)} %param.15) | copy-start | bytes 3538948
  5.0 85.4 %collective-permute-start = (bf16[2,18,6,384]{3,2,1,0:T(8,128)(2,1)}, bf16[2,18,6,384]{3,2,1,0:T(8,128)(2,1)}, u32[]{:S(2)}, u32[]{:S(2)}) collective-permute-start(bf16[2,18,6,384]{3,2,1,0:T(8,128)(2,1)} %slice.75), channel_id=1, source_target_pairs={{0,63},{1,0},{2,1},{3,2},{4,3},{5,4},{6,5},{7,6},{8,7},{9,8},{10,9... | collective-permute-start | bytes 497672 | tf_op jit(solution)/shard_map/ppermute | solution.py:17
  91.2 3.9 %collective-permute-start.1 = (bf16[2,3,24,384]{3,2,1,0:T(8,128)(2,1)S(1)}, bf16[2,3,24,384]{3,2,1,0:T(8,128)(2,1)S(1)}, u32[]{:S(2)}, u32[]{:S(2)}) collective-permute-start(bf16[2,3,24,384]{3,2,1,0:T(8,128)(2,1)S(1)} %pad_maximum_fusion.3), channel_id=1, source_target_pairs={{0,64},{64,0},{1,65},{65,1},{2,66},{66,2},{3,67},{67,3},{4,68},{68... | collective-permute-start | bytes 331784 | tf_op jit(solution)/shard_map/ppermute | solution.py:17
  123.7 6.8 %copy-start.2 = (bf16[384,384]{1,0:T(8,128)(2,1)S(1)}, bf16[384,384]{1,0:T(8,128)(2,1)}, u32[]{:S(2)}) copy-start(bf16[384,384]{1,0:T(8,128)(2,1)} %param.13) | copy-start | bytes 884740
  132.0 17.9 %copy-start.1 = (bf16[2,18,24,384]{3,2,1,0:T(8,128)(2,1)S(1)}, bf16[2,18,24,384]{3,2,1,0:T(8,128)(2,1)}, u32[]{:S(2)}) copy-start(bf16[2,18,24,384]{3,2,1,0:T(8,128)(2,1)} %param.8) | copy-start | bytes 1990660
  133.8 3.2 %collective-permute-start.2 = (bf16[2,3,24,384]{3,2,1,0:T(8,128)(2,1)S(1)}, bf16[2,3,24,384]{3,2,1,0:T(8,128)(2,1)S(1)}, u32[]{:S(2)}, u32[]{:S(2)}) collective-permute-start(bf16[2,3,24,384]{3,2,1,0:T(8,128)(2,1)S(1)} %slice.85), channel_id=1, source_target_pairs={{0,64},{64,0},{1,65},{65,1},{2,66},{66,2},{3,67},{67,3},{4,68},{68... | collective-permute-start | bytes 331784 | tf_op jit(solution)/shard_map/ppermute | solution.py:17
  137.0 12.9 %collective-permute-start.3 = (bf16[2,18,6,384]{3,2,1,0:T(8,128)(2,1)S(1)}, bf16[2,18,6,384]{3,2,1,0:T(8,128)(2,1)S(1)}, u32[]{:S(2)}, u32[]{:S(2)}) collective-permute-start(bf16[2,18,6,384]{3,2,1,0:T(8,128)(2,1)S(1)} %pad_maximum_fusion.2), channel_id=1, source_target_pairs={{0,1},{1,2},{2,3},{3,4},{4,5},{5,6},{6,7},{7,8},{8,9},{9,10},{10,1... | collective-permute-start | bytes 497672 | tf_op jit(solution)/shard_map/ppermute | solution.py:17
where the time goes:
time: 167 us; the launch traced here: 166 us
  local copies, waits for them, and re-layouts  81.5 us (49%)
  matrix products  36.7 us (22%)
  starting transfers between devices  21.8 us (13%)
  other arithmetic  13.9 us (8%)
  waiting for transfers between devices  11.7 us (7%)
    gather x3, local copies, waits for them, and re-layouts, bias_scores(): picked = jnp.take(flat_table, bias_index.reshape(-1), axis=1)  53.8 us
    ppermute x4, starting transfers between devices, from_behind(): return lax.ppermute(value, axis, pairs)  21.8 us
    dot_general x1, matrix products, feed_forward(): jnp.dot(hidden, w_fc2, preferred_element_type=jnp.float32)  14.9 us
    sub x1, matrix products, attend(): exponent = jnp.exp(scores - maxima)  11.8 us
    ppermute x4, waiting for transfers between devices, from_behind(): return lax.ppermute(value, axis, pairs)  11.7 us
    convert_element_type x1, local copies, waits for them, and re-layouts, bias_scores(): picked.astype(jnp.float32)  6.6 us
    slice x1, local copies, waits for them, and re-layouts, attend(): value_rows = packed[:, :, :, 2]  5.26 us
    dot_general x1, matrix products, attend(): jnp.einsum('abhij,abjhd->abihd', attn_weights, value_rows, preferred_elem...  4.93 us
  transfers between devices with their start and end apart: 4, of which 2 were waited for; matrix products, arithmetic and copies ran while one was open for 43% of the time, Pallas kernels for 0%

commit v1 on v0

v1 whole, which is shorter than its diff:
```python
import numpy as np
import jax
import jax.numpy as jnp
from jax import lax
from jax.experimental import pallas as pl
from jax.experimental.pallas import tpu as pltpu
from jax.sharding import PartitionSpec as P

F32 = jnp.float32
BF16 = jnp.bfloat16
EPS = 1e-05
LOG2E = 1.4426950408889634
C = 384
HEADS = 12
QUAD = 40
KEYS = 160
CHUNKS = 13
ROWS = 40
STRIDE = 40


def region_constants():
    lane = np.arange(512)
    p = lane % 256
    kk = p % 40
    valid = (p < 160) & (kk < 36)
    src_col = 12 * (lane // 256) + 6 * ((p % 80) // 40) + kk % 6
    lane_row = (kk // 18) * 6 + (p // 80) * 3 + (kk % 18) // 6
    cols = ((np.arange(24)[:, None] == src_col[None]) & valid[None]).astype(np.float32)
    row = np.arange(36)
    row_id = (row // 18) * 6 + row % 6
    keep = ((row_id[:, None] == lane_row[None]) & valid[None]).astype(np.float32)
    group = ((row[None] % 18) // 6 == np.arange(8)[:, None]).astype(np.float32)
    fill = np.where(valid, 0.0, -1.0).astype(np.float32)[None]
    return cols, keep, group, fill


def window_order(padded):
    spots = []
    for r2 in range(2):
        for c2 in range(2):
            for level in range(2):
                for r3 in range(3):
                    for c6 in range(6):
                        spots.append(level * 72 + (r2 * 3 + r3) * 12 + c2 * 6 + c6)
            if padded:
                spots += [-1] * 4
    return np.array(spots)


def index_constants(half):
    rows = window_order(False)[72 * half:72 * half + 72]
    pick = (rows[:, None] == np.arange(144)[None]).astype(np.float32)
    place = (np.arange(144)[:, None] == window_order(True)[None]).astype(np.float32)
    tile = (np.arange(32)[:, None] == (np.arange(256) % 32)[None]).astype(np.float32)
    keep = ((np.arange(72) % 8)[:, None] == (np.arange(256) // 32)[None]).astype(np.float32)
    gather = ((np.arange(72) // 8)[None] == np.arange(16)[:, None]).astype(np.float32)
    return pick, place, tile, keep, gather


def dot(a, b):
    return jnp.dot(a, b, preferred_element_type=F32)


def normalise(x):
    mean = jnp.mean(x, axis=-1, keepdims=True)
    centred = x - mean
    var = jnp.mean(centred * centred, axis=-1, keepdims=True)
    return (centred * lax.rsqrt(var + EPS)).astype(BF16)


def prep_body(fields, region, tab, cols, keep, group, fill, nq, comb, pay, xq):
    for cs in range(4):
        for rt in range(6):
            xq[rt, 40 * cs + 32:40 * cs + 40, :] = jnp.zeros((8, C), F32)

    def triple(rt, carry):
        for level in range(2):
            for r3 in range(3):
                x = fields[level * 18 + 3 * rt + r3].astype(F32)
                n = normalise(x).astype(F32)
                base = 6 * ((1 - level) * 3 + r3)
                for cs in range(4):
                    xq[rt, 40 * cs + base:40 * cs + base + 6, :] = n[6 * cs:6 * cs + 6, :]
        return carry

    lax.fori_loop(0, 6, triple, 0)
    reg = region[...].astype(F32).astype(BF16)
    spread = dot(reg, cols[...]) * keep[...]
    rows = dot(group[...], spread.astype(BF16)) + fill[...]
    comb[...] = rows
    nq[...] = xq[...].astype(BF16)
    pay[0:160, :] = xq[0].astype(BF16)
    pay[160:320, :] = xq[5].astype(BF16)
    last = jnp.concatenate([rows[2:3, 0:256], rows[2:3, 256:512], jnp.zeros((14, 256), F32)], axis=0)
    pay[320:336, 0:256] = last.astype(BF16)
    for c in range(CHUNKS):
        pay[336 + 16 * c:352 + 16 * c, 0:256] = tab[ROWS * c:ROWS * c + 16, :].astype(BF16)


def lon_body(nq, lat, comb, pay_r, pay_l, scr_r, scr_l):
    first = lat[160:320, :].astype(F32)
    final = lat[0:160, :].astype(F32)
    scr_r[0:40, :] = first[120:160, :]
    scr_l[0:40, :] = first[0:40, :]
    scr_r[280:320, :] = final[120:160, :]
    scr_l[280:320, :] = final[0:40, :]
    for rt in range(6):
        own = nq[rt].astype(F32)
        scr_r[40 * rt + 40:40 * rt + 80, :] = own[120:160, :]
        scr_l[40 * rt + 40:40 * rt + 80, :] = own[0:40, :]
    pay_r[0:320, :] = scr_r[...].astype(BF16)
    pay_l[...] = scr_l[...].astype(BF16)
    top = lat[320:336, 0:256].astype(F32)
    rows = jnp.concatenate([top[1:2, :], comb[0:3, 256:512], jnp.zeros((12, 256), F32)], axis=0)
    pay_r[320:336, 0:256] = rows.astype(BF16)


def bias_body(own_x, index, tab, swap, pick, place, tile, keep, gather, main, rem, tabs, lo_m, hi_m, lo_r, hi_r):
    for c in range(CHUNKS):
        tabs[ROWS * c:ROWS * c + ROWS, :] = tab[ROWS * c:ROWS * c + ROWS, :]
        if not own_x:
            tabs[ROWS * c:ROWS * c + 16, :] = swap[336 + 16 * c:352 + 16 * c, 0:256].astype(F32)
    idx = index[...]
    for part, m_ref, r_ref in ((idx & 255, lo_m, lo_r), (idx >> 8, hi_m, hi_r)):
        picked = dot(pick[...], part.astype(F32).astype(BF16)).astype(BF16)
        full = dot(picked, place[...])
        m_ref[...] = full[:, 0:128]
        wide = dot(full[:, 128:160].astype(BF16), tile[...]) * keep[...]
        r_ref[...] = dot(gather[...], wide.astype(BF16))
    table = tabs[...].astype(BF16)
    low = lax.broadcasted_iota(jnp.int32, (256, 256), 0).astype(F32)

    def look(lo, hi):
        hot = jnp.where(low == lo, 1.0, 0.0).astype(BF16)
        got = dot(table, hot)
        out = got[0:ROWS]
        for c in range(1, CHUNKS):
            out = jnp.where(hi == float(c), got[ROWS * c:ROWS * c + ROWS], out)
        return out * LOG2E

    def pair(step, carry):
        i = 2 * step
        lo = jnp.concatenate([lo_m[pl.ds(i, 1), :], lo_m[pl.ds(i + 1, 1), :]], axis=1)
        hi = jnp.concatenate([hi_m[pl.ds(i, 1), :], hi_m[pl.ds(i + 1, 1), :]], axis=1)
        out = look(lo, hi)
        spot = i + 4 * (i // 36)
        main[pl.ds(pl.multiple_of(spot * STRIDE, 8), ROWS), :] = out[:, 0:128]
        main[pl.ds(pl.multiple_of(spot * STRIDE + STRIDE, 8), ROWS), :] = out[:, 128:256]
        return carry

    lax.fori_loop(0, 36, pair, 0)

    def octet(g, carry):
        out = look(lo_r[pl.ds(g, 1), :], hi_r[pl.ds(g, 1), :])
        for q in range(8):
            i = 8 * g + q
            spot = i + 4 * (i // 36)
            piece = out[:, 128 * (q // 4):128 * (q // 4) + 128]
            if q % 4:
                piece = pltpu.roll(piece, 128 - 32 * (q % 4), axis=1)
            rem[pl.ds(pl.multiple_of(spot * STRIDE, 8), ROWS), :] = piece
        return carry

    lax.fori_loop(0, 9, octet, 0)


def main_body(fields, nq, lat, left, right, comb, bm1, br1, bm0, br0, w_qkv, w_proj, w_fc1, w_fc2, out,
              xs, kk, vv, qq, ctx, rows, res):
    def put(rt, cs, block):
        n = block.shape[0]
        xs[240 * rt + 40 * cs:240 * rt + 40 * cs + n, :] = block

    put(7, 1, lat[0:160, :].astype(F32))
    put(0, 1, lat[160:320, :].astype(F32))
    for rt in range(6):
        put(rt + 1, 1, nq[rt].astype(F32))
    lhalo = left[0:320, :].astype(F32)
    rhalo = right[...].astype(F32)
    for rt in range(8):
        put(rt, 0, lhalo[40 * rt:40 * rt + 40, :])
        put(rt, 5, rhalo[40 * rt:40 * rt + 40, :])

    def project(step, carry):
        at = pl.multiple_of(step * 480, 480)
        x = xs[pl.ds(at, 480), :].astype(BF16)
        y = dot(x, w_qkv[:, C:3 * C])
        kk[pl.ds(at, 480), :] = y[:, 0:C].astype(BF16)
        vv[pl.ds(at, 480), :] = y[:, C:2 * C].astype(BF16)
        return carry

    lax.fori_loop(0, 4, project, 0)
    for rt in range(6):
        qq[rt] = dot(nq[rt], w_qkv[:, 0:C]).astype(BF16).astype(F32)

    top = lat[320:336, 0:256].astype(F32)
    lreg = left[320:336, 0:256].astype(F32)
    rows[0:4, :] = lreg[0:4, :]
    rows[4:5, :] = top[0:1, :]
    rows[8:9, :] = top[1:2, :]
    rows[5:8, :] = comb[0:3, 0:256]
    rows[9:12, :] = comb[0:3, 256:512]

    lane = lax.broadcasted_iota(jnp.int32, (1, 128), 1)
    heads = [(lane // 32 == h) for h in range(4)]
    sub = lax.broadcasted_iota(jnp.int32, (8, KEYS), 0).astype(F32)
    ones = jnp.ones((KEYS, 128), BF16)
    scale = 32 ** -0.5 * LOG2E

    def unit(r2, step, carry):
        if r2:
            t, rt = step, 2 * step + 1
            th0 = jnp.where(step == 0, 0, 4 + 12 * step)
            bm, br = bm1, br1
        else:
            t, rt = step + 1, 2 * step + 2
            th0 = jnp.where(step == 2, 0, 16 + 12 * step)
            bm, br = bm0, br0
        for w, (c0, nrow, q0) in enumerate(((40, 40, 0), (0, 80, 40), (0, 40, 120))):
            ids = rows[pl.ds(4 * w + t, 1), :][:, 0:KEYS]
            hot = jnp.where(sub == ids, 1.0, 0.0).astype(BF16)
            same = lax.dot_general(hot, hot, (((0,), (0,)), ((), ())), preferred_element_type=F32)
            same = same[80 * r2 + c0:80 * r2 + c0 + nrow, :] > 0.5
            k0 = pl.multiple_of(480 * t + 80 * w, 80)
            k1 = pl.multiple_of(480 * t + 240 + 80 * w, 80)
            q_all = qq[rt - 1, q0:q0 + nrow, :]
            for g in range(3):
                sl = slice(128 * g, 128 * g + 128)
                k = jnp.concatenate([kk[pl.ds(k0, 80), sl], kk[pl.ds(k1, 80), sl]], axis=0)
                v = jnp.concatenate([vv[pl.ds(k0, 80), sl], vv[pl.ds(k1, 80), sl]], axis=0)
                q = q_all[:, sl]
                qs = jnp.concatenate([jnp.where(m, q, 0.0) for m in heads], axis=0).astype(BF16)
                s = lax.dot_general(qs, k, (((1,), (1,)), ((), ())), preferred_element_type=F32)
                parts = []
                for h in range(4):
                    at = c0 * STRIDE + th0 + 4 * g + h
                    b = jnp.concatenate([bm[pl.ds(at, nrow, stride=STRIDE), :],
                                         br[pl.ds(at, nrow, stride=STRIDE), :][:, 0:32]], axis=1)
                    x = s[h * nrow:(h + 1) * nrow, :] * scale + b
                    x = jnp.where(same, x, -1e30)
                    x = jnp.exp2(x - jnp.max(x, axis=1, keepdims=True))
                    parts.append(x.astype(BF16))
                p = jnp.concatenate(parts, axis=0)
                o = dot(p, jnp.concatenate([v, ones], axis=1))
                c = jnp.zeros((nrow, 128), F32)
                for h in range(4):
                    oh = o[h * nrow:(h + 1) * nrow, :]
                    c = jnp.where(heads[h], oh[:, 0:128] / oh[:, 128:256], c)
                ctx[rt - 1, q0:q0 + nrow, sl] = c
        return carry

    lax.fori_loop(0, 3, lambda s, c: unit(0, s, c), 0)
    lax.fori_loop(0, 3, lambda s, c: unit(1, s, c), 0)

    def back(rt, carry):
        att = dot(ctx[rt].astype(BF16), w_proj[...]).astype(BF16).astype(F32)
        qq[rt] = att
        for level in range(2):
            for r3 in range(3):
                base = 6 * ((1 - level) * 3 + r3)
                for cs in range(4):
                    res[level * 18 + 3 * rt + r3, 6 * cs:6 * cs + 6, :] = \
                        qq[rt, 40 * cs + base:40 * cs + base + 6, :]
        return carry

    lax.fori_loop(0, 6, back, 0)

    def feed(step, carry):
        x = fields[pl.ds(9 * step, 9)].astype(F32) + res[pl.ds(9 * step, 9)]
        x = x.reshape(216, C).astype(BF16).astype(F32)
        y = dot(normalise(x), w_fc1[...])
        hidden = (0.5 * y * (1.0 + lax.erf(y * (0.5 ** 0.5)))).astype(BF16)
        z = x + dot(hidden, w_fc2[...])
        out[pl.ds(9 * step, 9)] = z.reshape(9, 24, C).astype(BF16)
        return carry

    lax.fori_loop(0, 4, feed, 0)


def call(body, outs, scratch, args, limit=48, **kw):
    return pl.pallas_call(
        body,
        out_shape=outs,
        scratch_shapes=scratch,
        compiler_params=pltpu.CompilerParams(vmem_limit_bytes=limit << 20),
        **kw,
    )(*args)


def shift(value, axis, steps):
    count = lax.axis_size(axis)
    return lax.ppermute(value, axis, [(s, (s + steps) % count) for s in range(count)])


def sds(shape, dtype):
    return jax.ShapeDtypeStruct(shape, dtype)


def local(fields, region_ids, bias_index, earth_bias, w_qkv, w_proj, w_fc1, w_fc2):
    fields = fields.reshape(36, 24, C)
    region = region_ids.reshape(36, 24)
    eb = jnp.pad(earth_bias, ((0, 0), (0, 16), (0, 0))).reshape(3, CHUNKS, 256, HEADS)
    eb = eb.transpose(1, 0, 3, 2).astype(F32)
    tab = jnp.concatenate([jnp.pad(eb[:, 2], ((0, 0), (0, 4), (0, 0))), eb[:, 0], eb[:, 1]], axis=1)
    tab = tab.reshape(CHUNKS * ROWS, 256)
    cols, keep, group, fill = region_constants()
    nq, comb, pay = call(
        prep_body,
        (sds((6, 160, C), BF16), sds((8, 512), F32), sds((544, C), BF16)),
        [pltpu.VMEM((6, 160, C), F32)],
        (fields, region, tab, jnp.asarray(cols, BF16), jnp.asarray(keep, F32), jnp.asarray(group, BF16),
         jnp.asarray(fill, F32)),
    )
    lat = shift(pay, "lat", 1)

    def bias(half, swap):
        consts = index_constants(half)
        kinds = (BF16, BF16, BF16, F32, BF16)
        return call(
            lambda *refs: bias_body(half == 0, *refs),
            (sds((80 * STRIDE, 128), F32), sds((80 * STRIDE, 128), F32)),
            [pltpu.VMEM((CHUNKS * ROWS, 256), F32), pltpu.VMEM((72, 128), F32), pltpu.VMEM((72, 128), F32),
             pltpu.VMEM((16, 256), F32), pltpu.VMEM((16, 256), F32)],
            (bias_index, tab, swap) + tuple(jnp.asarray(c, k) for c, k in zip(consts, kinds)),
            cost_estimate=pl.CostEstimate(flops=4 * 10 ** 9, transcendentals=0, bytes_accessed=4 * 10 ** 6),
        )

    bm0, br0 = bias(0, pay)
    pay_r, pay_l = call(
        lon_body,
        (sds((336, C), BF16), sds((320, C), BF16)),
        [pltpu.VMEM((320, C), F32), pltpu.VMEM((320, C), F32)],
        (nq, lat, comb),
    )
    left = shift(pay_r, "lon", 1)
    right = shift(pay_l, "lon", -1)
    bm1, br1 = bias(1, lat)
    result = call(
        main_body,
        sds((36, 24, C), BF16),
        [pltpu.VMEM((1920, C), F32), pltpu.VMEM((1920, C), BF16), pltpu.VMEM((1920, C), BF16),
         pltpu.VMEM((6, 160, C), F32), pltpu.VMEM((6, 160, C), F32), pltpu.VMEM((16, 256), F32),
         pltpu.VMEM((36, 24, C), F32)],
        (fields, nq, lat, left, right, comb, bm1, br1, bm0, br0, w_qkv, w_proj, w_fc1, w_fc2),
    )
    return result.reshape(2, 18, 24, C)


def solution(mesh):
    return jax.shard_map(
        local,
        mesh=mesh,
        in_specs=(
            P("ens", "lat", "lon", None),
            P(None, "lat", "lon"),
            P(),
            P("lat", None, None),
            P(),
            P(),
            P(),
            P(),
        ),
        out_specs=P("ens", "lat", "lon", None),
        check_vma=False,
    )
```

time: 167 us -> 77.3 us (0.46)
  local copies, waits for them, and re-layouts: 81.5 us -> 6.67 us
  Pallas kernels: 0 us -> 49.4 us
  matrix products: 36.7 us -> 0 us
  other arithmetic: 13.9 us -> 1.06 us
  waiting for transfers between devices: 11.7 us -> 0.01 us
  starting transfers between devices: 21.8 us -> 19.5 us
    gather x3 -> x0, local copies, waits for them, and re-layouts: 53.8 us -> none  [bias_scores(): picked = jnp.take(flat_table, bias_index.reshape(-1), axis=1)]
    pallas_call x0 -> x5, Pallas kernels: none -> 49.4 us  [call(): pl.pallas_call(body, out_shape=outs, scratch_shapes=scratch, compiler_par...]
    dot_general x4 -> x0, matrix products: 24.9 us -> none  [the longest x1 14.9 us: feed_forward(): jnp.dot(hidden, w_fc2, preferred_element_type=jnp.float32)]
    sub x1 -> x0, matrix products: 11.8 us -> none  [attend(): exponent = jnp.exp(scores - maxima)]
    ppermute x4 -> x3, waiting for transfers between devices: 11.7 us -> 0.01 us  [shift(): lax.ppermute(value, axis, [(s, (s + steps) % count) for s in range(count)])]
    convert_element_type x3 -> x2, local copies, waits for them, and re-layouts: 10.7 us -> 0.47 us  [local(): eb = eb.transpose(1, 0, 3, 2).astype(F32)]
    reshape x9 -> x2, local copies, waits for them, and re-layouts: 9.55 us -> 0.73 us  [local(): region = region_ids.reshape(36, 24)]
    slice x10 -> x0, local copies, waits for them, and re-layouts: 6.63 us -> none  [the longest x1 5.26 us: attend(): value_rows = packed[:, :, :, 2]]
  transfers between devices with their start and end apart: 4 -> 3, of which waited for: 2 -> 0; matrix products, arithmetic and copies ran while one was open for 43% -> 0% of each run, Pallas kernels for 0% -> 33%
where the time goes in v1:
time: 77.3 us; the launch traced here: 77 us
  Pallas kernels  49.4 us (64%)
  starting transfers between devices  19.5 us (25%)
  local copies, waits for them, and re-layouts  6.67 us (9%)
  other arithmetic  1.06 us (1%)
    pallas_call x5, Pallas kernels, call(): pl.pallas_call(body, out_shape=outs, scratch_shapes=scratch, compiler_par...  49.4 us
    ppermute x3, starting transfers between devices, shift(): lax.ppermute(value, axis, [(s, (s + steps) % count) for s in range(count)])  19.5 us
    unnamed x40, local copies, waits for them, and re-layouts  5.43 us
  transfers between devices with their start and end apart: 3, of which 0 were waited for; matrix products, arithmetic and copies ran while one was open for 0% of the time, Pallas kernels for 33%

profile of v1, /device:TPU:1, one launch (start us, length us, event | category | flops | bytes accessed | tf_op | source)
XLA Modules:
  0.0 77.0 jit_solution(10522526104799581820)
XLA Ops:
  0.0 0.7 copy.28
  0.7 1.0 %pad_convert_fusion = f32[3,3328,12]{1,2,0:T(8,128)S(1)} fusion(bf16[3,3312,12]{1,2,0:T(8,128)(2,1)} %param.25), kind=kLoop, calls=%fused_computation.4 | loop fusion | flops 119808 | bytes 717696 | tf_op jit(solution)/shard_map/convert_element_type | solution.py:303
  1.7 0.2 reshape.19
  1.9 0.0 copy-start
  2.0 0.0 copy-start.9
  2.0 0.0 copy-start.10
  2.0 0.0 copy-start.11
  2.0 0.0 copy-start.12
  2.0 0.3 copy.31
  2.3 0.0 copy-start.13
  2.3 0.0 copy-start.14
  2.3 0.0 copy-start.15
  2.3 0.0 copy-start.17
  2.3 0.0 copy-start.18
  2.4 0.0 copy-start.19
  2.4 0.1 fusion
  2.5 0.6 copy-done
  3.0 1.6 %shard_map.208 = (bf16[6,160,384]{2,1,0:T(8,128)(2,1)S(1)}, f32[8,512]{1,0:T(8,128)S(1)}, bf16[544,384]{1,0:T(8,128)(2,1)S(1)}) custom-call(bf16[36,24,384]{2,1,0:T(8,128)(2,1)S(1)} %bitcast.14, s32[36,24]{1,0:T(8,128)S(1)} %reshape.20.region, f32[520,256]{1,0:T(8,128)S(1)} %bitcast.16, bf16[24,512]{1,0:T(8,128)(2,1)S(1)} %copy-done.10, ...), custom_call_target="tpu_custom_call" | custom-call | tf_op jit(solution)/shard_map/pallas_call | solution.py:281
  4.6 0.0 copy-start.16
  4.6 8.7 %collective-permute-start = (bf16[544,384]{1,0:T(8,128)(2,1)S(1)}, bf16[544,384]{1,0:T(8,128)(2,1)S(1)}, u32[]{:S(2)}, u32[]{:S(2)}) collective-permute-start(bf16[544,384]{1,0:T(8,128)(2,1)S(1)} %get-tuple-element.15.refs_2_), channel_id=1, source_target_pairs={{0,64},{64,0},{1,65},{65,1},{2,66},{66,2},{3,67},{67,3},{4,68},{68... | collective-permute-start | bytes 1253384 | tf_op jit(solution)/shard_map/ppermute | solution.py:292
  13.4 13.0 %shard_map.211 = (f32[3200,128]{1,0:T(8,128)S(1)}, f32[3200,128]{1,0:T(8,128)S(1)}) custom-call(s32[144,144]{1,0:T(8,128)S(1)} %copy-done.13, f32[520,256]{1,0:T(8,128)S(1)} %bitcast.17, bf16[544,384]{1,0:T(8,128)(2,1)S(1)} %get-tuple-element.15.refs_2_, bf16[72,144]{1,0:T(8,128)(2,1)S(1)} %copy-done.17, bf16[144,160]{1,0:T(8,128)(2,1)S(1)} %copy-done.15, ...), custom_call_target="tpu_custom_call" | custom-call | flops 4000000000 | bytes 4000000 | tf_op jit(solution)/shard_map/pallas_call | solution.py:281
  26.4 1.2 %copy-done.1 = f32[3200,128]{1,0:T(8,128)} copy-done((f32[3200,128]{1,0:T(8,128)}, f32[3200,128]{1,0:T(8,128)S(1)}, u32[]{:S(2)}) %copy-start.1) | copy-done | bytes 1638424
  27.6 1.2 %copy-done.2 = f32[3200,128]{1,0:T(8,128)} copy-done((f32[3200,128]{1,0:T(8,128)}, f32[3200,128]{1,0:T(8,128)S(1)}, u32[]{:S(2)}) %copy-start.2) | copy-done | bytes 1638424
  28.9 8.6 %collective-permute-start.2 = (bf16[320,384]{1,0:T(8,128)(2,1)S(1)}, bf16[320,384]{1,0:T(8,128)(2,1)S(1)}, u32[]{:S(2)}, u32[]{:S(2)}) collective-permute-start(bf16[320,384]{1,0:T(8,128)(2,1)S(1)} %get-tuple-element.18), channel_id=1, source_target_pairs={{0,63},{1,0},{2,1},{3,2},{4,3},{5,4},{6,5},{7,6},{8,7},{9,8},{10,9... | collective-permute-start | bytes 737288 | tf_op jit(solution)/shard_map/ppermute | solution.py:292
  37.5 0.0 copy-start.5
  37.5 0.0 copy-start.6
  37.5 0.0 copy-start.7
  37.5 2.2 %collective-permute-start.1 = (bf16[336,384]{1,0:T(8,128)(2,1)S(1)}, bf16[336,384]{1,0:T(8,128)(2,1)S(1)}, u32[]{:S(2)}, u32[]{:S(2)}) collective-permute-start(bf16[336,384]{1,0:T(8,128)(2,1)S(1)} %get-tuple-element.17), channel_id=1, source_target_pairs={{0,1},{1,2},{2,3},{3,4},{4,5},{5,6},{6,7},{7,8},{8,9},{9,10},{10,1... | collective-permute-start | bytes 774152 | tf_op jit(solution)/shard_map/ppermute | solution.py:292
  39.7 12.7 %shard_map.210 = (f32[3200,128]{1,0:T(8,128)S(1)}, f32[3200,128]{1,0:T(8,128)S(1)}) custom-call(s32[144,144]{1,0:T(8,128)S(1)} %copy-done.13, f32[520,256]{1,0:T(8,128)S(1)} %bitcast.18, bf16[544,384]{1,0:T(8,128)(2,1)S(1)} %collective-permute-done.lat.refs_2_, bf16[72,144]{1,0:T(8,128)(2,1)S(1)} %copy-done.16, bf16[144,160]{1,0:T(8,128)(2,1)S(1)} %copy-done.15, ...), custom_call_target="tpu_custom_call" | custom-call | flops 4000000000 | bytes 4000000 | tf_op jit(solution)/shard_map/pallas_call | solution.py:281
  52.4 1.2 %copy-done.3 = f32[3200,128]{1,0:T(8,128)} copy-done((f32[3200,128]{1,0:T(8,128)}, f32[3200,128]{1,0:T(8,128)S(1)}, u32[]{:S(2)}) %copy-start.3) | copy-done | bytes 1638424
  53.6 1.2 %copy-done.4 = f32[3200,128]{1,0:T(8,128)} copy-done((f32[3200,128]{1,0:T(8,128)}, f32[3200,128]{1,0:T(8,128)S(1)}, u32[]{:S(2)}) %copy-start.4) | copy-done | bytes 1638424
  54.9 22.1 %shard_map.212 = bf16[36,24,384]{2,1,0:T(8,128)(2,1)} custom-call(bf16[36,24,384]{2,1,0:T(8,128)(2,1)S(1)} %bitcast.15, bf16[6,160,384]{2,1,0:T(8,128)(2,1)S(1)} %get-tuple-element.14.nq, bf16[544,384]{1,0:T(8,128)(2,1)S(1)} %collective-permute-done.lat.refs_2_, bf16[336,384]{1,0:T(8,128)(2,1)S(1)} %collective-permute-done.1.left, ...), custom_call_target="tpu_custom_call" | custom-call | tf_op jit(solution)/shard_map/pallas_call | solution.py:281
  (26 shorter events, 0.1 us)
Async XLA Ops:
  1.9 1.1 %copy-start = (bf16[2,18,24,384]{3,2,1,0:T(8,128)(2,1)S(1)}, bf16[2,18,24,384]{3,2,1,0:T(8,128)(2,1)}, u32[]{:S(2)}) copy-start(bf16[2,18,24,384]{3,2,1,0:T(8,128)(2,1)} %param.22) | copy-start | bytes 1990660
  2.0 1.1 %copy-start.9 = (f32[36,512]{1,0:T(8,128)S(1)}, f32[36,512]{1,0:T(8,128)}, u32[]{:S(2)}) copy-start(f32[36,512]{1,0:T(8,128)} %constant.26.clone.keep) | copy-start | bytes 221188
  2.0 1.1 %copy-start.10 = (bf16[24,512]{1,0:T(8,128)(2,1)S(1)}, bf16[24,512]{1,0:T(8,128)(2,1)}, u32[]{:S(2)}) copy-start(bf16[24,512]{1,0:T(8,128)(2,1)} %constant.25.clone.cols) | copy-start | bytes 73732
  2.0 1.1 %copy-start.11 = (f32[1,512]{1,0:T(1,128)S(1)}, f32[1,512]{1,0:T(1,128)}, u32[]{:S(2)}) copy-start(f32[1,512]{1,0:T(1,128)} %constant.28.clone.fill) | copy-start | bytes 6148
  2.0 1.1 %copy-start.12 = (bf16[8,36]{1,0:T(8,128)(2,1)S(1)}, bf16[8,36]{1,0:T(8,128)(2,1)}, u32[]{:S(2)}) copy-start(bf16[8,36]{1,0:T(8,128)(2,1)} %constant.27.clone.group) | copy-start | bytes 1732
  2.3 11.1 %copy-start.13 = (s32[144,144]{1,0:T(8,128)S(1)}, s32[144,144]{1,0:T(8,128)}, u32[]{:S(2)}) copy-start(s32[144,144]{1,0:T(8,128)} %refs_0_.3) | copy-start | bytes 248836
  2.3 11.1 %copy-start.14 = (f32[72,256]{1,0:T(8,128)S(1)}, f32[72,256]{1,0:T(8,128)}, u32[]{:S(2)}) copy-start(f32[72,256]{1,0:T(8,128)} %constant.32.clone.refs_6_) | copy-start | bytes 221188
  2.3 11.1 %copy-start.15 = (bf16[144,160]{1,0:T(8,128)(2,1)S(1)}, bf16[144,160]{1,0:T(8,128)(2,1)}, u32[]{:S(2)}) copy-start(bf16[144,160]{1,0:T(8,128)(2,1)} %constant.30.clone.refs_4_) | copy-start | bytes 138244
  2.3 11.1 %copy-start.17 = (bf16[72,144]{1,0:T(8,128)(2,1)S(1)}, bf16[72,144]{1,0:T(8,128)(2,1)}, u32[]{:S(2)}) copy-start(bf16[72,144]{1,0:T(8,128)(2,1)} %constant.29.clone.refs_3_) | copy-start | bytes 62212
  2.3 11.1 %copy-start.18 = (bf16[32,256]{1,0:T(8,128)(2,1)S(1)}, bf16[32,256]{1,0:T(8,128)(2,1)}, u32[]{:S(2)}) copy-start(bf16[32,256]{1,0:T(8,128)(2,1)} %constant.31.clone.refs_5_) | copy-start | bytes 49156
  2.4 11.1 %copy-start.19 = (bf16[16,72]{1,0:T(8,128)(2,1)S(1)}, bf16[16,72]{1,0:T(8,128)(2,1)}, u32[]{:S(2)}) copy-start(bf16[16,72]{1,0:T(8,128)(2,1)} %constant.33.clone.refs_7_) | copy-start | bytes 6916
  4.6 35.1 %copy-start.16 = (bf16[72,144]{1,0:T(8,128)(2,1)S(1)}, bf16[72,144]{1,0:T(8,128)(2,1)}, u32[]{:S(2)}) copy-start(bf16[72,144]{1,0:T(8,128)(2,1)} %constant.34.clone.refs_3_) | copy-start | bytes 62212
  4.6 24.2 %collective-permute-start = (bf16[544,384]{1,0:T(8,128)(2,1)S(1)}, bf16[544,384]{1,0:T(8,128)(2,1)S(1)}, u32[]{:S(2)}, u32[]{:S(2)}) collective-permute-start(bf16[544,384]{1,0:T(8,128)(2,1)S(1)} %get-tuple-element.15.refs_2_), channel_id=1, source_target_pairs={{0,64},{64,0},{1,65},{65,1},{2,66},{66,2},{3,67},{67,3},{4,68},{68... | collective-permute-start | bytes 1253384 | tf_op jit(solution)/shard_map/ppermute | solution.py:292
  26.4 1.2 %copy-start.1 = (f32[3200,128]{1,0:T(8,128)}, f32[3200,128]{1,0:T(8,128)S(1)}, u32[]{:S(2)}) copy-start(f32[3200,128]{1,0:T(8,128)S(1)} %get-tuple-element.21.bm0) | copy-start | bytes 4915204
  27.6 1.2 %copy-start.2 = (f32[3200,128]{1,0:T(8,128)}, f32[3200,128]{1,0:T(8,128)S(1)}, u32[]{:S(2)}) copy-start(f32[3200,128]{1,0:T(8,128)S(1)} %get-tuple-element.22.br0) | copy-start | bytes 4915204
  28.9 25.9 %collective-permute-start.2 = (bf16[320,384]{1,0:T(8,128)(2,1)S(1)}, bf16[320,384]{1,0:T(8,128)(2,1)S(1)}, u32[]{:S(2)}, u32[]{:S(2)}) collective-permute-start(bf16[320,384]{1,0:T(8,128)(2,1)S(1)} %get-tuple-element.18), channel_id=1, source_target_pairs={{0,63},{1,0},{2,1},{3,2},{4,3},{5,4},{6,5},{7,6},{8,7},{9,8},{10,9... | collective-permute-start | bytes 737288 | tf_op jit(solution)/shard_map/ppermute | solution.py:292
  37.5 17.4 %copy-start.5 = (bf16[384,1536]{1,0:T(8,128)(2,1)S(1)}, bf16[384,1536]{1,0:T(8,128)(2,1)}, u32[]{:S(2)}) copy-start(bf16[384,1536]{1,0:T(8,128)(2,1)} %w_fc1.1) | copy-start | bytes 3538948
  37.5 17.4 %copy-start.6 = (bf16[1536,384]{1,0:T(8,128)(2,1)S(1)}, bf16[1536,384]{1,0:T(8,128)(2,1)}, u32[]{:S(2)}) copy-start(bf16[1536,384]{1,0:T(8,128)(2,1)} %w_fc2.1) | copy-start | bytes 3538948
  37.5 17.4 %copy-start.7 = (bf16[384,1152]{1,0:T(8,128)(2,1)S(1)}, bf16[384,1152]{1,0:T(8,128)(2,1)}, u32[]{:S(2)}) copy-start(bf16[384,1152]{1,0:T(8,128)(2,1)} %w_qkv.1) | copy-start | bytes 2654212
  37.5 17.4 %copy-start.8 = (bf16[384,384]{1,0:T(8,128)(2,1)S(1)}, bf16[384,384]{1,0:T(8,128)(2,1)}, u32[]{:S(2)}) copy-start(bf16[384,384]{1,0:T(8,128)(2,1)} %w_proj.1) | copy-start | bytes 884740
  37.5 17.3 %collective-permute-start.1 = (bf16[336,384]{1,0:T(8,128)(2,1)S(1)}, bf16[336,384]{1,0:T(8,128)(2,1)S(1)}, u32[]{:S(2)}, u32[]{:S(2)}) collective-permute-start(bf16[336,384]{1,0:T(8,128)(2,1)S(1)} %get-tuple-element.17), channel_id=1, source_target_pairs={{0,1},{1,2},{2,3},{3,4},{4,5},{5,6},{6,7},{7,8},{8,9},{9,10},{10,1... | collective-permute-start | bytes 774152 | tf_op jit(solution)/shard_map/ppermute | solution.py:292
  52.4 1.2 %copy-start.3 = (f32[3200,128]{1,0:T(8,128)}, f32[3200,128]{1,0:T(8,128)S(1)}, u32[]{:S(2)}) copy-start(f32[3200,128]{1,0:T(8,128)S(1)} %get-tuple-element.19.bm1) | copy-start | bytes 4915204
  53.6 1.2 %copy-start.4 = (f32[3200,128]{1,0:T(8,128)}, f32[3200,128]{1,0:T(8,128)S(1)}, u32[]{:S(2)}) copy-start(f32[3200,128]{1,0:T(8,128)S(1)} %get-tuple-element.20.br1) | copy-start | bytes 4915204

commit v2 on v1

v2 whole, which is shorter than its diff:
```python
import numpy as np
import jax
import jax.numpy as jnp
from jax import lax
from jax.experimental import pallas as pl
from jax.experimental.pallas import tpu as pltpu
from jax.sharding import PartitionSpec as P

F32 = jnp.float32
BF16 = jnp.bfloat16
EPS = 1e-05
LOG2E = 1.4426950408889634
C = 384
HEADS = 12
QUAD = 40
KEYS = 160
POSITIONS = 3312
CHUNKS = 13
ROWS = 40
SPAN = 80


def floor_div(x, d):
    return jnp.floor((x + 0.5) * (1.0 / d))


def region_constants():
    lane = lax.broadcasted_iota(jnp.int32, (1, 512), 1).astype(F32)
    w = floor_div(lane, 256)
    p = lane - 256 * w
    r2 = floor_div(p, 80)
    c2 = floor_div(p - 80 * r2, 40)
    kk = p - 80 * r2 - 40 * c2
    valid = (p < 160) & (kk < 36)
    level = floor_div(kk, 18)
    r3 = floor_div(kk - 18 * level, 6)
    src = jnp.where(valid, 12 * w + 6 * c2 + kk - 18 * level - 6 * r3, -1.0)
    lane_row = jnp.where(valid, level * 6 + r2 * 3 + r3, -1.0)
    cols = jnp.where(lax.broadcasted_iota(jnp.int32, (24, 512), 0).astype(F32) == src, 1.0, 0.0)
    row = lax.broadcasted_iota(jnp.int32, (36, 1), 0).astype(F32)
    r = floor_div(row, 2)
    row_id = (row - 2 * r) * 6 + r - 6 * floor_div(r, 6)
    keep = jnp.where(row_id == lane_row, 1.0, 0.0)
    at = floor_div(lax.broadcasted_iota(jnp.int32, (1, 36), 1).astype(F32), 12)
    group = jnp.where(lax.broadcasted_iota(jnp.int32, (8, 36), 0).astype(F32) == at, 1.0, 0.0)
    return cols.astype(BF16), keep, group.astype(BF16), jnp.where(valid, 0.0, -1.0)


def spread_table(eb, c):
    n = min(256, POSITIONS - 256 * c)
    got = eb[:, 256 * c:256 * c + n].astype(F32)
    if n < 256:
        got = jnp.concatenate([got, jnp.zeros((HEADS, 256 - n), F32)], axis=1)
    return got


def window_order(padded):
    spots = []
    for r2 in range(2):
        for c2 in range(2):
            for level in range(2):
                for r3 in range(3):
                    for c6 in range(6):
                        spots.append(level * 72 + (r2 * 3 + r3) * 12 + c2 * 6 + c6)
            if padded:
                spots += [-1] * 4
    return np.array(spots)


def index_constants():
    pick = (window_order(False)[:, None] == np.arange(144)[None]).astype(np.float32)
    place = (np.arange(144)[:, None] == window_order(True)[None]).astype(np.float32)
    tile = (np.arange(32)[:, None] == (np.arange(256) % 32)[None]).astype(np.float32)
    keep = ((np.arange(144) % 8)[:, None] == (np.arange(256) // 32)[None]).astype(np.float32)
    row = np.arange(144)
    gather = ((16 * (row // 72) + row % 72 // 8)[None] == np.arange(32)[:, None]).astype(np.float32)
    return pick, place, tile, keep, gather


def dot(a, b):
    return jnp.dot(a, b, preferred_element_type=F32)


def normalise(x):
    mean = jnp.mean(x, axis=-1, keepdims=True)
    centred = x - mean
    var = jnp.mean(centred * centred, axis=-1, keepdims=True)
    return (centred * lax.rsqrt(var + EPS)).astype(BF16)


def fetch_all(pairs, sems):
    copies = [pltpu.make_async_copy(a, b, sems.at[n]) for n, (a, b) in enumerate(pairs)]
    for copy in copies:
        copy.start()
    return copies


def prep_body(fields_hbm, region_hbm, eb_hbm, nq, comb, pay, own, xq, reg, fields, region, eb, sems):
    copies = fetch_all(((fields_hbm, fields), (region_hbm, region), (eb_hbm.at[2], eb)), sems)
    for cs in range(4):
        for rt in range(6):
            xq[rt, 40 * cs + 32:40 * cs + 40, :] = jnp.zeros((8, C), F32)

    copies[0].wait()

    def triple(rt, carry):
        for level in range(2):
            for r3 in range(3):
                x = fields[level * 18 + 3 * rt + r3].astype(F32)
                n = normalise(x).astype(F32)
                base = 6 * ((1 - level) * 3 + r3)
                for cs in range(4):
                    xq[rt, 40 * cs + base:40 * cs + base + 6, :] = n[6 * cs:6 * cs + 6, :]
        return carry

    lax.fori_loop(0, 6, triple, 0)
    copies[1].wait()
    for r in range(18):
        reg[2 * r:2 * r + 2, :] = region[r].astype(F32)
    cols, keep, group, fill = region_constants()
    spread = dot(reg[...].astype(BF16), cols) * keep
    rows = dot(group, spread.astype(BF16)) + fill
    comb[...] = rows
    nq[...] = xq[...].astype(BF16)
    pay[0:160, :] = xq[0].astype(BF16)
    pay[160:320, :] = xq[5].astype(BF16)
    last = jnp.concatenate([rows[2:3, 0:256], rows[2:3, 256:512], jnp.zeros((14, 256), F32)], axis=0)
    pay[320:336, 0:256] = last.astype(BF16)
    copies[2].wait()
    for c in range(CHUNKS):
        own[c] = jnp.concatenate([spread_table(eb, c), jnp.zeros((4, 256), F32)], axis=0)
        pay[336 + 16 * c:352 + 16 * c, 0:256] = own[c].astype(BF16)


def lon_body(nq, lat, comb, pay_r, pay_l, scr_r, scr_l):
    first = lat[160:320, :].astype(F32)
    final = lat[0:160, :].astype(F32)
    scr_r[0:40, :] = first[120:160, :]
    scr_l[0:40, :] = first[0:40, :]
    scr_r[280:320, :] = final[120:160, :]
    scr_l[280:320, :] = final[0:40, :]
    for rt in range(6):
        own = nq[rt].astype(F32)
        scr_r[40 * rt + 40:40 * rt + 80, :] = own[120:160, :]
        scr_l[40 * rt + 40:40 * rt + 80, :] = own[0:40, :]
    pay_r[0:320, :] = scr_r[...].astype(BF16)
    pay_l[...] = scr_l[...].astype(BF16)
    top = lat[320:336, 0:256].astype(F32)
    rows = jnp.concatenate([top[1:2, :], comb[0:3, 256:512], jnp.zeros((12, 256), F32)], axis=0)
    pay_r[320:336, 0:256] = rows.astype(BF16)


def index_body(index_hbm, eb_hbm, *refs):
    consts, (lo_m, hi_m, lo_r, hi_r, inner, index, eb), bufs, sems = refs[:5], refs[5:12], refs[12:17], refs[17]
    copies = fetch_all(((index_hbm, index),) + tuple(zip(consts, bufs)) + ((eb_hbm.at[0:2], eb),), sems)
    for copy in copies[:6]:
        copy.wait()
    pick, place, tile, keep, gather = bufs
    idx = index[...]
    for part, m_ref, r_ref in ((idx & 255, lo_m, lo_r), (idx >> 8, hi_m, hi_r)):
        picked = dot(pick[...], part.astype(F32).astype(BF16)).astype(BF16)
        full = dot(picked, place[...])
        m_ref[...] = full[:, 0:128]
        wide = dot(full[:, 128:160].astype(BF16), tile[...]) * keep[...]
        r_ref[...] = dot(gather[...], wide.astype(BF16))
    copies[6].wait()
    for c in range(CHUNKS):
        inner[c, 0:12, :] = spread_table(eb.at[0], c)
        inner[c, 12:24, :] = spread_table(eb.at[1], c)


def bias_body(lo_m, hi_m, lo_r, hi_r, own, inner, swap, main0, rem0, main1, rem1, tabs):
    low = lax.broadcasted_iota(jnp.int32, (256, 256), 0).astype(F32)

    def look(table, lo, hi):
        hot = jnp.where(low == lo, 1.0, 0.0).astype(BF16)
        got = dot(table, hot)
        out = got[0:ROWS]
        for c in range(1, CHUNKS):
            out = jnp.where(hi == float(c), got[ROWS * c:ROWS * c + ROWS], out)
        return out * LOG2E

    for c in range(CHUNKS):
        tabs[ROWS * c + 16:ROWS * c + ROWS, :] = inner[c]

    for half, main, rem in ((0, main0, rem0), (1, main1, rem1)):
        for c in range(CHUNKS):
            tabs[ROWS * c:ROWS * c + 16, :] = \
                swap[336 + 16 * c:352 + 16 * c, 0:256].astype(F32) if half else own[c]
        table = tabs[...].astype(BF16)

        def pair(step, carry):
            i = 2 * step
            at = 72 * half + i
            lo = jnp.concatenate([lo_m[pl.ds(at, 1), :], lo_m[pl.ds(at + 1, 1), :]], axis=1)
            hi = jnp.concatenate([hi_m[pl.ds(at, 1), :], hi_m[pl.ds(at + 1, 1), :]], axis=1)
            out = look(table, lo, hi)
            spot = i + 4 * (i // 36)
            main[pl.ds(spot, ROWS, stride=SPAN), :] = out[:, 0:128]
            main[pl.ds(spot + 1, ROWS, stride=SPAN), :] = out[:, 128:256]
            return carry

        lax.fori_loop(0, 36, pair, 0, unroll=12)

        def octet(g, carry):
            out = look(table, lo_r[pl.ds(16 * half + g, 1), :], hi_r[pl.ds(16 * half + g, 1), :])
            for q in range(8):
                i = 8 * g + q
                spot = i + 4 * (i // 36)
                piece = out[:, 128 * (q // 4):128 * (q // 4) + 128]
                if q % 4:
                    piece = pltpu.roll(piece, 128 - 32 * (q % 4), axis=1)
                rem[pl.ds(spot, ROWS, stride=SPAN), :] = piece
            return carry

        lax.fori_loop(0, 9, octet, 0, unroll=9)


def main_body(fields, nq, lat, left, right, comb, bm1, br1, bm0, br0, w_qkv, w_proj, w_fc1, w_fc2, out,
              xs, kk, vv, qq, ctx, rows, res, qf, kf, sc, mx):
    def put(rt, cs, block):
        n = block.shape[0]
        xs[240 * rt + 40 * cs:240 * rt + 40 * cs + n, :] = block

    put(7, 1, lat[0:160, :].astype(F32))
    put(0, 1, lat[160:320, :].astype(F32))
    for rt in range(6):
        put(rt + 1, 1, nq[rt].astype(F32))
    lhalo = left[0:320, :].astype(F32)
    rhalo = right[...].astype(F32)
    for rt in range(8):
        put(rt, 0, lhalo[40 * rt:40 * rt + 40, :])
        put(rt, 5, rhalo[40 * rt:40 * rt + 40, :])

    def project(step, carry):
        at = pl.multiple_of(step * 480, 480)
        x = xs[pl.ds(at, 480), :].astype(BF16)
        y = dot(x, w_qkv[:, C:3 * C])
        kk[pl.ds(at, 480), :] = y[:, 0:C].astype(BF16)
        vv[pl.ds(at, 480), :] = y[:, C:2 * C].astype(BF16)
        return carry

    lax.fori_loop(0, 4, project, 0, unroll=4)
    for rt in range(6):
        qq[rt] = dot(nq[rt], w_qkv[:, 0:C]).astype(BF16).astype(F32)

    top = lat[320:336, 0:256].astype(F32)
    lreg = left[320:336, 0:256].astype(F32)
    rows[0:4, :] = lreg[0:4, :]
    rows[4:5, :] = top[0:1, :]
    rows[8:9, :] = top[1:2, :]
    rows[5:8, :] = comb[0:3, 0:256]
    rows[9:12, :] = comb[0:3, 256:512]

    lane = lax.broadcasted_iota(jnp.int32, (1, 128), 1)
    heads = [(lane // 32 == h) for h in range(4)]
    rows[12:16, :] = jnp.full((4, 256), -1.0, F32)
    sub = lax.broadcasted_iota(jnp.int32, (8, KEYS), 0).astype(F32)
    hot = jnp.concatenate([jnp.where(sub == rows[n:n + 1, 0:KEYS], 1.0, 0.0) for n in range(16)], axis=0)
    eye = lax.broadcasted_iota(jnp.int32, (128, 128), 0) == lax.broadcasted_iota(jnp.int32, (128, 128), 1)
    seen = lax.dot_general(hot.astype(BF16), jnp.where(eye, 1.0, 0.0).astype(BF16), (((0,), (0,)), ((), ())),
                           preferred_element_type=F32)
    qf[...] = seen
    kf[...] = (seen - 1.0) * 1e30
    ones = jnp.ones((KEYS, 128), BF16)
    scale = 32 ** -0.5 * LOG2E
    spans = ((40, 40, 0), (0, 80, 40), (0, 40, 120))

    def places(r2, step):
        return (step, 2 * step + 1) if r2 else (step + 1, 2 * step + 2)

    def window(ref, t, w, sl):
        k0 = pl.multiple_of(480 * t + 80 * w, 80)
        k1 = pl.multiple_of(480 * t + 240 + 80 * w, 80)
        return jnp.concatenate([ref[pl.ds(k0, 80), sl], ref[pl.ds(k1, 80), sl]], axis=0)

    def score(r2, step):
        t, rt = places(r2, step)
        if r2:
            th0 = jnp.where(step == 0, 0, 4 + 12 * step)
            bm, br = bm1, br1
        else:
            th0 = jnp.where(step == 2, 0, 16 + 12 * step)
            bm, br = bm0, br0
        for w, (c0, nrow, q0) in enumerate(spans):
            far = jnp.where(lane // 8 == 4 * w + t, kf[...], 0.0).astype(BF16)
            near = qf[80 * r2 + c0:80 * r2 + c0 + nrow, :]
            for g in range(3):
                sl = slice(128 * g, 128 * g + 128)
                k = jnp.concatenate([window(kk, t, w, sl), far], axis=1)
                q = qq[rt - 1, q0:q0 + nrow, sl]
                qs = jnp.concatenate([jnp.concatenate([jnp.where(m, q, 0.0), near], axis=1) for m in heads],
                                     axis=0).astype(BF16)
                at = 640 * g + 4 * q0
                s = lax.dot_general(qs, k, (((1,), (1,)), ((), ())), preferred_element_type=F32)
                for h in range(4):
                    th = pl.multiple_of((th0 + 4 * g + h) * SPAN, SPAN) + c0
                    b = jnp.concatenate([bm[pl.ds(th, nrow), :], br[pl.ds(th, nrow), :][:, 0:32]], axis=1)
                    x = s[h * nrow:(h + 1) * nrow, :] * scale + b
                    sc[r2, at + h * nrow:at + (h + 1) * nrow, :] = x
                    mx[r2, at + h * nrow:at + (h + 1) * nrow, :] = jnp.broadcast_to(
                        jnp.max(x, axis=1, keepdims=True), (nrow, 128))

    def attend(r2, step):
        t, rt = places(r2, step)
        for w, (c0, nrow, q0) in enumerate(spans):
            for g in range(3):
                sl = slice(128 * g, 128 * g + 128)
                at = 640 * g + 4 * q0
                parts = []
                for h in range(4):
                    x = sc[r2, at + h * nrow:at + (h + 1) * nrow, :]
                    m = mx[r2, at + h * nrow:at + (h + 1) * nrow, :]
                    x = x - jnp.concatenate([m, m[:, 0:32]], axis=1)
                    parts.append(jnp.exp2(x).astype(BF16))
                o = dot(jnp.concatenate(parts, axis=0), jnp.concatenate([window(vv, t, w, sl), ones], axis=1))
                os = [o[h * nrow:(h + 1) * nrow, :] for h in range(4)]
                num, den = os[3][:, 0:128], os[3][:, 128:256]
                for h in range(3):
                    num = jnp.where(heads[h], os[h][:, 0:128], num)
                    den = jnp.where(heads[h], os[h][:, 128:256], den)
                ctx[rt - 1, q0:q0 + nrow, sl] = num / den

    score(0, 0)

    def steps(step, carry):
        score(1, step)
        attend(0, step)
        score(0, jnp.minimum(step + 1, 2))
        attend(1, step)
        return carry

    lax.fori_loop(0, 3, steps, 0)

    def back(rt, carry):
        att = dot(ctx[rt].astype(BF16), w_proj[...]).astype(BF16).astype(F32)
        qq[rt] = att
        for level in range(2):
            for r3 in range(3):
                base = 6 * ((1 - level) * 3 + r3)
                for cs in range(4):
                    res[level * 18 + 3 * rt + r3, 6 * cs:6 * cs + 6, :] = \
                        qq[rt, 40 * cs + base:40 * cs + base + 6, :]
        return carry

    lax.fori_loop(0, 6, back, 0, unroll=6)

    def feed(step, carry):
        x = fields[pl.ds(9 * step, 9)].astype(F32) + res[pl.ds(9 * step, 9)]
        x = x.reshape(216, C).astype(BF16).astype(F32)
        y = dot(normalise(x), w_fc1[...])
        hidden = (0.5 * y * (1.0 + lax.erf(y * (0.5 ** 0.5)))).astype(BF16)
        z = x + dot(hidden, w_fc2[...])
        out[pl.ds(9 * step, 9)] = z.reshape(9, 24, C).astype(BF16)
        return carry

    lax.fori_loop(0, 4, feed, 0, unroll=4)


def call(body, outs, scratch, args, limit=28, **kw):
    return pl.pallas_call(
        body,
        out_shape=outs,
        scratch_shapes=scratch,
        compiler_params=pltpu.CompilerParams(vmem_limit_bytes=limit << 20),
        **kw,
    )(*args)


def hold(x):
    return pltpu.with_memory_space_constraint(x, pltpu.HBM)


def shift(value, axis, steps):
    count = lax.axis_size(axis)
    return lax.ppermute(value, axis, [(s, (s + steps) % count) for s in range(count)])


def sds(shape, dtype):
    return jax.ShapeDtypeStruct(shape, dtype)


def local(fields, region_ids, bias_index, earth_bias, w_qkv, w_proj, w_fc1, w_fc2):
    fields = fields.reshape(36, 24, C)
    region = region_ids.transpose(1, 0, 2)
    tables = earth_bias.transpose(0, 2, 1)
    nq, comb, pay, own = call(
        prep_body,
        (sds((6, 160, C), BF16), sds((8, 512), F32), sds((544, C), BF16), sds((CHUNKS, 16, 256), F32)),
        [pltpu.VMEM((6, 160, C), F32), pltpu.VMEM((36, 24), F32), pltpu.VMEM((36, 24, C), BF16),
         pltpu.VMEM((18, 2, 24), jnp.int32), pltpu.VMEM((HEADS, POSITIONS), BF16), pltpu.SemaphoreType.DMA((3,))],
        tuple(hold(x) for x in (fields, region, tables)),
        in_specs=[pl.BlockSpec(memory_space=pltpu.HBM)] * 3,
    )
    lat = shift(pay, "lat", 1)

    kinds = (BF16, BF16, BF16, F32, BF16)
    consts = tuple(jnp.asarray(c, k) for c, k in zip(index_constants(), kinds))
    *found, inner = call(
        index_body,
        (sds((144, 128), F32), sds((144, 128), F32), sds((32, 256), F32), sds((32, 256), F32),
         sds((CHUNKS, 24, 256), F32)),
        [pltpu.VMEM((144, 144), jnp.int32), pltpu.VMEM((2, HEADS, POSITIONS), BF16)] +
        [pltpu.VMEM(c.shape, c.dtype) for c in consts] + [pltpu.SemaphoreType.DMA((7,))],
        tuple(hold(x) for x in (bias_index, tables) + consts),
        in_specs=[pl.BlockSpec(memory_space=pltpu.HBM)] * 7,
        cost_estimate=pl.CostEstimate(flops=10 ** 9, transcendentals=0, bytes_accessed=10 ** 6),
    )
    pay_r, pay_l = call(
        lon_body,
        (sds((336, C), BF16), sds((320, C), BF16)),
        [pltpu.VMEM((320, C), F32), pltpu.VMEM((320, C), F32)],
        (nq, lat, comb),
    )
    left = shift(pay_r, "lon", 1)
    right = shift(pay_l, "lon", -1)
    bm0, br0, bm1, br1 = call(
        bias_body,
        (sds((ROWS * SPAN, 128), F32),) * 4,
        [pltpu.VMEM((CHUNKS * ROWS, 256), F32)],
        tuple(found) + (own, inner, lat),
        cost_estimate=pl.CostEstimate(flops=10 ** 10, transcendentals=0, bytes_accessed=8 * 10 ** 6),
    )
    result = call(
        main_body,
        sds((36, 24, C), BF16),
        [pltpu.VMEM((1920, C), F32), pltpu.VMEM((1920, C), BF16), pltpu.VMEM((1920, C), BF16),
         pltpu.VMEM((6, 160, C), F32), pltpu.VMEM((6, 160, C), F32), pltpu.VMEM((16, 256), F32),
         pltpu.VMEM((36, 24, C), F32), pltpu.VMEM((KEYS, 128), F32), pltpu.VMEM((KEYS, 128), F32),
         pltpu.VMEM((2, 1920, KEYS), F32),
         pltpu.VMEM((2, 1920, 128), F32)],
        (fields, nq, lat, left, right, comb, bm1, br1, bm0, br0, w_qkv, w_proj, w_fc1, w_fc2),
    )
    return result.reshape(2, 18, 24, C)


def solution(mesh):
    return jax.shard_map(
        local,
        mesh=mesh,
        in_specs=(
            P("ens", "lat", "lon", None),
            P(None, "lat", "lon"),
            P(),
            P("lat", None, None),
            P(),
            P(),
            P(),
            P(),
        ),
        out_specs=P("ens", "lat", "lon", None),
        check_vma=False,
    )
```

time: 77.3 us -> 46.5 us (0.60)
  Pallas kernels: 49.4 us -> 26.9 us
  local copies, waits for them, and re-layouts: 6.67 us -> 0.03 us
  other arithmetic: 1.06 us -> 0 us
    pallas_call x5, Pallas kernels: 49.4 us -> 26.9 us  [call(): pl.pallas_call(body, out_shape=outs, scratch_shapes=scratch, compiler_par...]
    unnamed x40 -> x10, local copies, waits for them, and re-layouts: 5.43 us -> 0.03 us
    convert_element_type x1 -> x0, other arithmetic: 1.01 us -> none  [local(): eb = eb.transpose(1, 0, 3, 2).astype(F32)]
  transfers between devices with their start and end apart: 3 -> 3, of which waited for: 0 -> 0; matrix products, arithmetic and copies ran while one was open for 0% -> 0% of each run, Pallas kernels for 33% -> 25%
where the time goes in v2:
time: 46.5 us; the launch traced here: 46.3 us
  Pallas kernels  26.9 us (58%)
  starting transfers between devices  19.2 us (41%)
    pallas_call x5, Pallas kernels, call(): pl.pallas_call(body, out_shape=outs, scratch_shapes=scratch, compiler_par...  26.9 us
    ppermute x3, starting transfers between devices, shift(): lax.ppermute(value, axis, [(s, (s + steps) % count) for s in range(count)])  19.2 us
  transfers between devices with their start and end apart: 3, of which 0 were waited for; matrix products, arithmetic and copies ran while one was open for 0% of the time, Pallas kernels for 25%

profile of v2, /device:TPU:1, one launch (start us, length us, event | category | flops | bytes accessed | tf_op | source)
XLA Modules:
  0.0 46.3 jit_solution(2604461923957205662)
XLA Ops:
  0.0 2.8 %shard_map.127 = (bf16[6,160,384]{2,1,0:T(8,128)(2,1)S(1)}, f32[8,512]{1,0:T(8,128)S(1)}, bf16[544,384]{1,0:T(8,128)(2,1)S(1)}, f32[13,16,256]{2,1,0:T(8,128)S(1)}) custom-call(bf16[36,24,384]{2,1,0:T(8,128)(2,1)} %bitcast.4, s32[18,2,24]{2,1,0:T(2,128)} %bitcast.8, bf16[3,12,3312]{2,1,0:T(8,128)(2,1)} %bitcast.6), custom_call_target="tpu_custom_call" | custom-call | tf_op jit(solution)/shard_map/pallas_call | solution.py:361
  2.8 8.7 %collective-permute-start = (bf16[544,384]{1,0:T(8,128)(2,1)S(1)}, bf16[544,384]{1,0:T(8,128)(2,1)S(1)}, u32[]{:S(2)}, u32[]{:S(2)}) collective-permute-start(bf16[544,384]{1,0:T(8,128)(2,1)S(1)} %get-tuple-element.21), channel_id=1, source_target_pairs={{0,64},{64,0},{1,65},{65,1},{2,66},{66,2},{3,67},{67,3},{4,68},{68... | collective-permute-start | bytes 1253384 | tf_op jit(solution)/shard_map/ppermute | solution.py:376
  11.5 2.1 %shard_map.129 = (f32[144,128]{1,0:T(8,128)S(1)}, f32[144,128]{1,0:T(8,128)S(1)}, f32[32,256]{1,0:T(8,128)S(1)}, f32[32,256]{1,0:T(8,128)S(1)}, f32[13,24,256]{2,1,0:T(8,128)S(1)}) custom-call(s32[144,144]{1,0:T(8,128)} %index_hbm.1, bf16[3,12,3312]{2,1,0:T(8,128)(2,1)} %bitcast.7, bf16[144,144]{1,0:T(8,128)(2,1)} %constant.10.clone.refs_0_, ...), custom_call_target="tpu_custom_call" | custom-call | flops 1000000000 | bytes 1000000 | tf_op jit(solution)/shard_map/pallas_call | solution.py:361
  13.7 0.0 collective-permute-done.lat.swap
  13.7 1.9 %collective-permute-start.1 = (bf16[336,384]{1,0:T(8,128)(2,1)S(1)}, bf16[336,384]{1,0:T(8,128)(2,1)S(1)}, u32[]{:S(2)}, u32[]{:S(2)}) collective-permute-start(bf16[336,384]{1,0:T(8,128)(2,1)S(1)} %get-tuple-element.23), channel_id=1, source_target_pairs={{0,1},{1,2},{2,3},{3,4},{4,5},{5,6},{6,7},{7,8},{8,9},{9,10},{10,1... | collective-permute-start | bytes 774152 | tf_op jit(solution)/shard_map/ppermute | solution.py:376
  15.6 8.5 %collective-permute-start.2 = (bf16[320,384]{1,0:T(8,128)(2,1)S(1)}, bf16[320,384]{1,0:T(8,128)(2,1)S(1)}, u32[]{:S(2)}, u32[]{:S(2)}) collective-permute-start(bf16[320,384]{1,0:T(8,128)(2,1)S(1)} %get-tuple-element.24), channel_id=1, source_target_pairs={{0,63},{1,0},{2,1},{3,2},{4,3},{5,4},{6,5},{7,6},{8,7},{9,8},{10,9... | collective-permute-start | bytes 737288 | tf_op jit(solution)/shard_map/ppermute | solution.py:376
  24.2 0.0 copy-start
  24.2 0.0 copy-start.1
  24.2 0.0 copy-start.2
  24.2 0.0 copy-start.3
  24.2 0.0 copy-start.4
  24.2 9.6 %shard_map.130 = (f32[3200,128]{1,0:T(8,128)S(1)}, f32[3200,128]{1,0:T(8,128)S(1)}, f32[3200,128]{1,0:T(8,128)S(1)}, f32[3200,128]{1,0:T(8,128)S(1)}) custom-call(f32[144,128]{1,0:T(8,128)S(1)} %get-tuple-element.25.lo_m, f32[144,128]{1,0:T(8,128)S(1)} %get-tuple-element.26.hi_m, f32[32,256]{1,0:T(8,128)S(1)} %get-tuple-element.27.lo_r, ...), custom_call_target="tpu_custom_call" | custom-call | flops 10000000000 | bytes 8000000 | tf_op jit(solution)/shard_map/pallas_call | solution.py:361
  33.9 0.0 collective-permute-done.2.right
  33.9 0.0 collective-permute-done.1.left
  33.9 0.0 copy-done
  33.9 0.0 copy-done.1
  33.9 0.0 copy-done.2
  33.9 0.0 copy-done.3
  33.9 0.0 copy-done.4
  33.9 12.4 %shard_map.131 = bf16[36,24,384]{2,1,0:T(8,128)(2,1)} custom-call(bf16[36,24,384]{2,1,0:T(8,128)(2,1)S(1)} %bitcast.5, bf16[6,160,384]{2,1,0:T(8,128)(2,1)S(1)} %get-tuple-element.20.nq, bf16[544,384]{1,0:T(8,128)(2,1)S(1)} %collective-permute-done.lat.swap, bf16[336,384]{1,0:T(8,128)(2,1)S(1)} %collective-permute-done.1.left, ...), custom_call_target="tpu_custom_call" | custom-call | tf_op jit(solution)/shard_map/pallas_call | solution.py:361
  (1 shorter events, 0.0 us)
Async XLA Ops:
  2.8 10.9 %collective-permute-start = (bf16[544,384]{1,0:T(8,128)(2,1)S(1)}, bf16[544,384]{1,0:T(8,128)(2,1)S(1)}, u32[]{:S(2)}, u32[]{:S(2)}) collective-permute-start(bf16[544,384]{1,0:T(8,128)(2,1)S(1)} %get-tuple-element.21), channel_id=1, source_target_pairs={{0,64},{64,0},{1,65},{65,1},{2,66},{66,2},{3,67},{67,3},{4,68},{68... | collective-permute-start | bytes 1253384 | tf_op jit(solution)/shard_map/ppermute | solution.py:376
  13.7 20.2 %collective-permute-start.1 = (bf16[336,384]{1,0:T(8,128)(2,1)S(1)}, bf16[336,384]{1,0:T(8,128)(2,1)S(1)}, u32[]{:S(2)}, u32[]{:S(2)}) collective-permute-start(bf16[336,384]{1,0:T(8,128)(2,1)S(1)} %get-tuple-element.23), channel_id=1, source_target_pairs={{0,1},{1,2},{2,3},{3,4},{4,5},{5,6},{6,7},{7,8},{8,9},{9,10},{10,1... | collective-permute-start | bytes 774152 | tf_op jit(solution)/shard_map/ppermute | solution.py:376
  15.6 18.2 %collective-permute-start.2 = (bf16[320,384]{1,0:T(8,128)(2,1)S(1)}, bf16[320,384]{1,0:T(8,128)(2,1)S(1)}, u32[]{:S(2)}, u32[]{:S(2)}) collective-permute-start(bf16[320,384]{1,0:T(8,128)(2,1)S(1)} %get-tuple-element.24), channel_id=1, source_target_pairs={{0,63},{1,0},{2,1},{3,2},{4,3},{5,4},{6,5},{7,6},{8,7},{9,8},{10,9... | collective-permute-start | bytes 737288 | tf_op jit(solution)/shard_map/ppermute | solution.py:376
  24.2 9.7 %copy-start = (bf16[2,18,24,384]{3,2,1,0:T(8,128)(2,1)S(1)}, bf16[2,18,24,384]{3,2,1,0:T(8,128)(2,1)}, u32[]{:S(2)}) copy-start(bf16[2,18,24,384]{3,2,1,0:T(8,128)(2,1)} %param.13) | copy-start | bytes 1990660
  24.2 9.7 %copy-start.1 = (bf16[384,1536]{1,0:T(8,128)(2,1)S(1)}, bf16[384,1536]{1,0:T(8,128)(2,1)}, u32[]{:S(2)}) copy-start(bf16[384,1536]{1,0:T(8,128)(2,1)} %w_fc1.1) | copy-start | bytes 3538948
  24.2 9.7 %copy-start.2 = (bf16[1536,384]{1,0:T(8,128)(2,1)S(1)}, bf16[1536,384]{1,0:T(8,128)(2,1)}, u32[]{:S(2)}) copy-start(bf16[1536,384]{1,0:T(8,128)(2,1)} %w_fc2.1) | copy-start | bytes 3538948
  24.2 9.7 %copy-start.3 = (bf16[384,1152]{1,0:T(8,128)(2,1)S(1)}, bf16[384,1152]{1,0:T(8,128)(2,1)}, u32[]{:S(2)}) copy-start(bf16[384,1152]{1,0:T(8,128)(2,1)} %w_qkv.1) | copy-start | bytes 2654212
  24.2 9.7 %copy-start.4 = (bf16[384,384]{1,0:T(8,128)(2,1)S(1)}, bf16[384,384]{1,0:T(8,128)(2,1)}, u32[]{:S(2)}) copy-start(bf16[384,384]{1,0:T(8,128)(2,1)} %w_proj.1) | copy-start | bytes 884740

commit v3 on v2

--- a/solution.py
+++ b/solution.py
@@ -12,7 +12,6 @@
 LOG2E = 1.4426950408889634
 C = 384
 HEADS = 12
-QUAD = 40
 KEYS = 160
 POSITIONS = 3312
 CHUNKS = 13
@@ -113,7 +112,7 @@
                     xq[rt, 40 * cs + base:40 * cs + base + 6, :] = n[6 * cs:6 * cs + 6, :]
         return carry
 
-    lax.fori_loop(0, 6, triple, 0)
+    lax.fori_loop(0, 6, triple, 0, unroll=3)
     copies[1].wait()
     for r in range(18):
         reg[2 * r:2 * r + 2, :] = region[r].astype(F32)
@@ -132,22 +131,24 @@
         pay[336 + 16 * c:352 + 16 * c, 0:256] = own[c].astype(BF16)
 
 
-def lon_body(nq, lat, comb, pay_r, pay_l, scr_r, scr_l):
-    first = lat[160:320, :].astype(F32)
-    final = lat[0:160, :].astype(F32)
-    scr_r[0:40, :] = first[120:160, :]
-    scr_l[0:40, :] = first[0:40, :]
-    scr_r[280:320, :] = final[120:160, :]
-    scr_l[280:320, :] = final[0:40, :]
+def column(nq, lat, scr, cs):
+    sl = slice(40 * cs, 40 * cs + 40)
+    scr[0:40, :] = lat[160:320, :].astype(F32)[sl, :]
+    scr[280:320, :] = lat[0:160, :].astype(F32)[sl, :]
     for rt in range(6):
-        own = nq[rt].astype(F32)
-        scr_r[40 * rt + 40:40 * rt + 80, :] = own[120:160, :]
-        scr_l[40 * rt + 40:40 * rt + 80, :] = own[0:40, :]
-    pay_r[0:320, :] = scr_r[...].astype(BF16)
-    pay_l[...] = scr_l[...].astype(BF16)
+        scr[40 * rt + 40:40 * rt + 80, :] = nq[rt].astype(F32)[sl, :]
+    return scr[...].astype(BF16)
+
+
+def right_body(nq, lat, comb, pay, scr):
+    pay[0:320, :] = column(nq, lat, scr, 3)
     top = lat[320:336, 0:256].astype(F32)
     rows = jnp.concatenate([top[1:2, :], comb[0:3, 256:512], jnp.zeros((12, 256), F32)], axis=0)
-    pay_r[320:336, 0:256] = rows.astype(BF16)
+    pay[320:336, 0:256] = rows.astype(BF16)
+
+
+def left_body(nq, lat, after, pay, scr):
+    pay[...] = column(nq, lat, scr, 0)
 
 
 def index_body(index_hbm, eb_hbm, *refs):
@@ -169,8 +170,14 @@
         inner[c, 12:24, :] = spread_table(eb.at[1], c)
 
 
-def bias_body(lo_m, hi_m, lo_r, hi_r, own, inner, swap, main0, rem0, main1, rem1, tabs):
+def early_blocks():
+    return jnp.maximum(7 - lax.axis_index("lon") % 32, 0)
+
+
+def bias_body(late, lo_m, hi_m, lo_r, hi_r, own, inner, swap, *refs):
+    main0, rem0, main1, rem1, tabs = refs[4:] if late else refs
     low = lax.broadcasted_iota(jnp.int32, (256, 256), 0).astype(F32)
+    early = early_blocks()
 
     def look(table, lo, hi):
         hot = jnp.where(low == lo, 1.0, 0.0).astype(BF16)
@@ -188,138 +195,131 @@
             tabs[ROWS * c:ROWS * c + 16, :] = \
                 swap[336 + 16 * c:352 + 16 * c, 0:256].astype(F32) if half else own[c]
         table = tabs[...].astype(BF16)
-
-        def pair(step, carry):
-            i = 2 * step
-            at = 72 * half + i
-            lo = jnp.concatenate([lo_m[pl.ds(at, 1), :], lo_m[pl.ds(at + 1, 1), :]], axis=1)
-            hi = jnp.concatenate([hi_m[pl.ds(at, 1), :], hi_m[pl.ds(at + 1, 1), :]], axis=1)
-            out = look(table, lo, hi)
-            spot = i + 4 * (i // 36)
-            main[pl.ds(spot, ROWS, stride=SPAN), :] = out[:, 0:128]
-            main[pl.ds(spot + 1, ROWS, stride=SPAN), :] = out[:, 128:256]
+        done = jnp.clip(early - 4 * half, 0, 4)
+
+        def pairs(block, carry):
+            first = 24 * block
+            for step in range(12):
+                at = 72 * half + first + 2 * step
+                lo = jnp.concatenate([lo_m[pl.ds(at, 1), :], lo_m[pl.ds(at + 1, 1), :]], axis=1)
+                hi = jnp.concatenate([hi_m[pl.ds(at, 1), :], hi_m[pl.ds(at + 1, 1), :]], axis=1)
+                out = look(table, lo, hi)
+                spot = first + 2 * step
+                spot = spot + jnp.where(spot >= 36, 4, 0)
+                main[pl.ds(spot, ROWS, stride=SPAN), :] = out[:, 0:128]
+                main[pl.ds(spot + 1, ROWS, stride=SPAN), :] = out[:, 128:256]
             return carry
 
-        lax.fori_loop(0, 36, pair, 0, unroll=12)
-
-        def octet(g, carry):
-            out = look(table, lo_r[pl.ds(16 * half + g, 1), :], hi_r[pl.ds(16 * half + g, 1), :])
-            for q in range(8):
-                i = 8 * g + q
-                spot = i + 4 * (i // 36)
-                piece = out[:, 128 * (q // 4):128 * (q // 4) + 128]
-                if q % 4:
-                    piece = pltpu.roll(piece, 128 - 32 * (q % 4), axis=1)
-                rem[pl.ds(spot, ROWS, stride=SPAN), :] = piece
-            return carry
-
-        lax.fori_loop(0, 9, octet, 0, unroll=9)
-
-
-def main_body(fields, nq, lat, left, right, comb, bm1, br1, bm0, br0, w_qkv, w_proj, w_fc1, w_fc2, out,
-              xs, kk, vv, qq, ctx, rows, res, qf, kf, sc, mx):
-    def put(rt, cs, block):
-        n = block.shape[0]
-        xs[240 * rt + 40 * cs:240 * rt + 40 * cs + n, :] = block
-
-    put(7, 1, lat[0:160, :].astype(F32))
-    put(0, 1, lat[160:320, :].astype(F32))
-    for rt in range(6):
-        put(rt + 1, 1, nq[rt].astype(F32))
-    lhalo = left[0:320, :].astype(F32)
-    rhalo = right[...].astype(F32)
-    for rt in range(8):
-        put(rt, 0, lhalo[40 * rt:40 * rt + 40, :])
-        put(rt, 5, rhalo[40 * rt:40 * rt + 40, :])
-
+        if late:
+            lax.fori_loop(jnp.minimum(done, 3), 3, pairs, 0)
+        else:
+            lax.fori_loop(0, jnp.minimum(done, 3), pairs, 0)
+
+        @pl.when(done < 4 if late else done >= 4)
+        def _():
+            for g in range(9):
+                out = look(table, lo_r[16 * half + g:16 * half + g + 1, :], hi_r[16 * half + g:16 * half + g + 1, :])
+                for q in range(8):
+                    i = 8 * g + q
+                    spot = i + 4 * (i // 36)
+                    piece = out[:, 128 * (q // 4):128 * (q // 4) + 128]
+                    if q % 4:
+                        piece = pltpu.roll(piece, 128 - 32 * (q % 4), axis=1)
+                    rem[pl.ds(spot, ROWS, stride=SPAN), :] = piece
+
+
+SPANS = ((40, 40, 0), (0, 80, 40), (0, 40, 120))
+SCALE = 32 ** -0.5 * LOG2E
+
+
+def head_lanes():
+    lane = lax.broadcasted_iota(jnp.int32, (1, 128), 1)
+    return lane, [(lane // 32 == h) for h in range(4)]
+
+
+def put(xs, group, rt, second, block):
+    at = 640 * group + 80 * rt + 40 * second
+    xs[at:at + block.shape[0], :] = block
+
+
+def key_values(xs, kk, vv, w_qkv, count):
     def project(step, carry):
-        at = pl.multiple_of(step * 480, 480)
-        x = xs[pl.ds(at, 480), :].astype(BF16)
-        y = dot(x, w_qkv[:, C:3 * C])
-        kk[pl.ds(at, 480), :] = y[:, 0:C].astype(BF16)
-        vv[pl.ds(at, 480), :] = y[:, C:2 * C].astype(BF16)
+        at = pl.multiple_of(step * 320, 320)
+        y = dot(xs[pl.ds(at, 320), :].astype(BF16), w_qkv[:, C:3 * C])
+        kk[pl.ds(at, 320), :] = y[:, 0:C].astype(BF16)
+        vv[pl.ds(at, 320), :] = y[:, C:2 * C].astype(BF16)
         return carry
 
-    lax.fori_loop(0, 4, project, 0, unroll=4)
-    for rt in range(6):
-        qq[rt] = dot(nq[rt], w_qkv[:, 0:C]).astype(BF16).astype(F32)
-
-    top = lat[320:336, 0:256].astype(F32)
-    lreg = left[320:336, 0:256].astype(F32)
-    rows[0:4, :] = lreg[0:4, :]
-    rows[4:5, :] = top[0:1, :]
-    rows[8:9, :] = top[1:2, :]
-    rows[5:8, :] = comb[0:3, 0:256]
-    rows[9:12, :] = comb[0:3, 256:512]
-
-    lane = lax.broadcasted_iota(jnp.int32, (1, 128), 1)
-    heads = [(lane // 32 == h) for h in range(4)]
-    rows[12:16, :] = jnp.full((4, 256), -1.0, F32)
+    lax.fori_loop(0, count, project, 0, unroll=count)
+
+
+def region_features(rows, qf, kf):
     sub = lax.broadcasted_iota(jnp.int32, (8, KEYS), 0).astype(F32)
-    hot = jnp.concatenate([jnp.where(sub == rows[n:n + 1, 0:KEYS], 1.0, 0.0) for n in range(16)], axis=0)
-    eye = lax.broadcasted_iota(jnp.int32, (128, 128), 0) == lax.broadcasted_iota(jnp.int32, (128, 128), 1)
-    seen = lax.dot_general(hot.astype(BF16), jnp.where(eye, 1.0, 0.0).astype(BF16), (((0,), (0,)), ((), ())),
-                           preferred_element_type=F32)
+    hot = jnp.concatenate([jnp.where(sub == rows[n:n + 1, 0:KEYS], 1.0, 0.0) for n in range(8)], axis=0)
+    eye = lax.broadcasted_iota(jnp.int32, (64, 128), 0) == lax.broadcasted_iota(jnp.int32, (64, 128), 1)
+    seen = lax.dot_general(
+        jnp.concatenate([hot, jnp.zeros((64, KEYS), F32)], axis=0).astype(BF16),
+        jnp.concatenate([jnp.where(eye, 1.0, 0.0), jnp.zeros((64, 128), F32)], axis=0).astype(BF16),
+        (((0,), (0,)), ((), ())), preferred_element_type=F32)
     qf[...] = seen
     kf[...] = (seen - 1.0) * 1e30
+
+
+def attention(windows, tables, qq, kk, vv, qf, kf, sc, mx, store):
+    lane, heads = head_lanes()
     ones = jnp.ones((KEYS, 128), BF16)
-    scale = 32 ** -0.5 * LOG2E
-    spans = ((40, 40, 0), (0, 80, 40), (0, 40, 120))
 
     def places(r2, step):
         return (step, 2 * step + 1) if r2 else (step + 1, 2 * step + 2)
-
-    def window(ref, t, w, sl):
-        k0 = pl.multiple_of(480 * t + 80 * w, 80)
-        k1 = pl.multiple_of(480 * t + 240 + 80 * w, 80)
-        return jnp.concatenate([ref[pl.ds(k0, 80), sl], ref[pl.ds(k1, 80), sl]], axis=0)
 
     def score(r2, step):
         t, rt = places(r2, step)
         if r2:
             th0 = jnp.where(step == 0, 0, 4 + 12 * step)
-            bm, br = bm1, br1
         else:
             th0 = jnp.where(step == 2, 0, 16 + 12 * step)
-            bm, br = bm0, br0
-        for w, (c0, nrow, q0) in enumerate(spans):
-            far = jnp.where(lane // 8 == 4 * w + t, kf[...], 0.0).astype(BF16)
+        bm, br = tables[r2]
+        top = 0
+        for n, w in enumerate(windows):
+            c0, nrow, q0 = SPANS[w]
+            far = jnp.where(lane // 8 == 4 * n + t, kf[...], 0.0).astype(BF16)
             near = qf[80 * r2 + c0:80 * r2 + c0 + nrow, :]
             for g in range(3):
                 sl = slice(128 * g, 128 * g + 128)
-                k = jnp.concatenate([window(kk, t, w, sl), far], axis=1)
+                k = jnp.concatenate([kk[pl.ds(pl.multiple_of(640 * n + 160 * t, 160), KEYS), sl], far], axis=1)
                 q = qq[rt - 1, q0:q0 + nrow, sl]
                 qs = jnp.concatenate([jnp.concatenate([jnp.where(m, q, 0.0), near], axis=1) for m in heads],
                                      axis=0).astype(BF16)
-                at = 640 * g + 4 * q0
                 s = lax.dot_general(qs, k, (((1,), (1,)), ((), ())), preferred_element_type=F32)
                 for h in range(4):
                     th = pl.multiple_of((th0 + 4 * g + h) * SPAN, SPAN) + c0
                     b = jnp.concatenate([bm[pl.ds(th, nrow), :], br[pl.ds(th, nrow), :][:, 0:32]], axis=1)
-                    x = s[h * nrow:(h + 1) * nrow, :] * scale + b
-                    sc[r2, at + h * nrow:at + (h + 1) * nrow, :] = x
-                    mx[r2, at + h * nrow:at + (h + 1) * nrow, :] = jnp.broadcast_to(
-                        jnp.max(x, axis=1, keepdims=True), (nrow, 128))
+                    x = s[h * nrow:(h + 1) * nrow, :] * SCALE + b
+                    sc[r2, top:top + nrow, :] = x
+                    mx[r2, top:top + nrow, :] = jnp.broadcast_to(jnp.max(x, axis=1, keepdims=True), (nrow, 128))
+                    top += nrow
 
     def attend(r2, step):
         t, rt = places(r2, step)
-        for w, (c0, nrow, q0) in enumerate(spans):
+        top = 0
+        for n, w in enumerate(windows):
+            _, nrow, _ = SPANS[w]
             for g in range(3):
                 sl = slice(128 * g, 128 * g + 128)
-                at = 640 * g + 4 * q0
                 parts = []
-                for h in range(4):
-                    x = sc[r2, at + h * nrow:at + (h + 1) * nrow, :]
-                    m = mx[r2, at + h * nrow:at + (h + 1) * nrow, :]
-                    x = x - jnp.concatenate([m, m[:, 0:32]], axis=1)
+                for _ in range(4):
+                    m = mx[r2, top:top + nrow, :]
+                    x = sc[r2, top:top + nrow, :] - jnp.concatenate([m, m[:, 0:32]], axis=1)
                     parts.append(jnp.exp2(x).astype(BF16))
-                o = dot(jnp.concatenate(parts, axis=0), jnp.concatenate([window(vv, t, w, sl), ones], axis=1))
+                    top += nrow
+                v = vv[pl.ds(pl.multiple_of(640 * n + 160 * t, 160), KEYS), sl]
+                o = dot(jnp.concatenate(parts, axis=0), jnp.concatenate([v, ones], axis=1))
                 os = [o[h * nrow:(h + 1) * nrow, :] for h in range(4)]
                 num, den = os[3][:, 0:128], os[3][:, 128:256]
                 for h in range(3):
                     num = jnp.where(heads[h], os[h][:, 0:128], num)
                     den = jnp.where(heads[h], os[h][:, 128:256], den)
-                ctx[rt - 1, q0:q0 + nrow, sl] = num / den
+                store(rt - 1, w, sl, num / den)
 
     score(0, 0)
 
@@ -332,15 +332,63 @@
 
     lax.fori_loop(0, 3, steps, 0)
 
+
+def inner_body(nq, lat, comb, bm1, br1, bm0, br0, w_qkv, qq, ctx, xs, kk, vv, rows, qf, kf, sc, mx):
+    xs[0:80, :] = lat[200:280, :].astype(F32)
+    xs[560:640, :] = lat[0:160, :].astype(F32)[40:120, :]
+    for rt in range(6):
+        xs[80 * rt + 80:80 * rt + 160, :] = nq[rt].astype(F32)[40:120, :]
+    key_values(xs, kk, vv, w_qkv, 2)
+    for rt in range(6):
+        qq[rt] = dot(nq[rt], w_qkv[:, 0:C]).astype(BF16).astype(F32)
+    rows[...] = jnp.full((8, 256), -1.0, F32)
+    rows[0:1, :] = lat[320:336, 0:256].astype(F32)[0:1, :]
+    rows[1:4, :] = comb[0:3, 0:256]
+    region_features(rows, qf, kf)
+
+    def store(rt, w, sl, value):
+        ctx[rt, :, sl] = value
+
+    attention((1,), ((bm0, br0), (bm1, br1)), qq, kk, vv, qf, kf, sc, mx, store)
+
+
+def outer_body(fields, nq, lat, left, right, comb, qq, mid, bm1, br1, bm0, br0, w_qkv, w_proj, w_fc1, w_fc2, out,
+               xs, kk, vv, ctx, att, rows, res, qf, kf, sc, mx):
+    below = lat[0:160, :].astype(F32)
+    above = lat[160:320, :].astype(F32)
+    put(xs, 0, 0, 1, above[0:40, :])
+    put(xs, 1, 0, 0, above[120:160, :])
+    put(xs, 0, 7, 1, below[0:40, :])
+    put(xs, 1, 7, 0, below[120:160, :])
+    lhalo = left[0:320, :].astype(F32)
+    rhalo = right[...].astype(F32)
+    for rt in range(8):
+        put(xs, 0, rt, 0, lhalo[40 * rt:40 * rt + 40, :])
+        put(xs, 1, rt, 1, rhalo[40 * rt:40 * rt + 40, :])
+    for rt in range(6):
+        own = nq[rt].astype(F32)
+        put(xs, 0, rt + 1, 1, own[0:40, :])
+        put(xs, 1, rt + 1, 0, own[120:160, :])
+        ctx[rt, 40:120, :] = mid[rt]
+    key_values(xs, kk, vv, w_qkv, 4)
+    rows[0:4, :] = left[320:336, 0:256].astype(F32)[0:4, :]
+    rows[4:5, :] = lat[320:336, 0:256].astype(F32)[1:2, :]
+    rows[5:8, :] = comb[0:3, 256:512]
+    region_features(rows, qf, kf)
+
+    def store(rt, w, sl, value):
+        ctx[rt, SPANS[w][2]:SPANS[w][2] + 40, sl] = value
+
+    attention((0, 2), ((bm0, br0), (bm1, br1)), qq, kk, vv, qf, kf, sc, mx, store)
+
     def back(rt, carry):
-        att = dot(ctx[rt].astype(BF16), w_proj[...]).astype(BF16).astype(F32)
-        qq[rt] = att
+        att[rt] = dot(ctx[rt].astype(BF16), w_proj[...]).astype(BF16).astype(F32)
         for level in range(2):
             for r3 in range(3):
                 base = 6 * ((1 - level) * 3 + r3)
                 for cs in range(4):
                     res[level * 18 + 3 * rt + r3, 6 * cs:6 * cs + 6, :] = \
-                        qq[rt, 40 * cs + base:40 * cs + base + 6, :]
+                        att[rt, 40 * cs + base:40 * cs + base + 6, :]
         return carry
 
     lax.fori_loop(0, 6, back, 0, unroll=6)
@@ -406,30 +454,46 @@
         in_specs=[pl.BlockSpec(memory_space=pltpu.HBM)] * 7,
         cost_estimate=pl.CostEstimate(flops=10 ** 9, transcendentals=0, bytes_accessed=10 ** 6),
     )
-    pay_r, pay_l = call(
-        lon_body,
-        (sds((336, C), BF16), sds((320, C), BF16)),
-        [pltpu.VMEM((320, C), F32), pltpu.VMEM((320, C), F32)],
-        (nq, lat, comb),
+
+    def bias(late, extra):
+        return call(
+            lambda *refs: bias_body(late, *refs),
+            (sds((ROWS * SPAN, 128), F32),) * 4,
+            [pltpu.VMEM((CHUNKS * ROWS, 256), F32)],
+            tuple(found) + (own, inner, lat) + extra,
+            cost_estimate=pl.CostEstimate(flops=10 ** 10, transcendentals=0,
+                                          bytes_accessed=8 * 10 ** 6),
+            input_output_aliases={7 + n: n for n in range(4)} if late else {},
+        )
+
+    pay_r = call(right_body, sds((336, C), BF16), [pltpu.VMEM((320, C), F32)], (nq, lat, comb))
+    left = shift(pay_r, "lon", 1)
+    some = bias(False, ())
+    pay_l = call(
+        left_body,
+        sds((320, C), BF16),
+        [pltpu.VMEM((320, C), F32)],
+        (nq, lat, some[0]),
+        in_specs=[pl.BlockSpec(memory_space=pltpu.VMEM)] * 2 + [pl.BlockSpec(memory_space=pl.ANY)],
     )
-    left = shift(pay_r, "lon", 1)
     right = shift(pay_l, "lon", -1)
-    bm0, br0, bm1, br1 = call(
-        bias_body,
-        (sds((ROWS * SPAN, 128), F32),) * 4,
-        [pltpu.VMEM((CHUNKS * ROWS, 256), F32)],
-        tuple(found) + (own, inner, lat),
-        cost_estimate=pl.CostEstimate(flops=10 ** 10, transcendentals=0, bytes_accessed=8 * 10 ** 6),
+    bm0, br0, bm1, br1 = bias(True, tuple(some))
+    vm = pltpu.VMEM
+    work = [vm((8, 256), F32), vm((KEYS, 128), F32), vm((KEYS, 128), F32)]
+    qq, mid = call(
+        inner_body,
+        (sds((6, 160, C), F32), sds((6, SPAN, C), F32)),
+        [vm((640, C), F32), vm((640, C), BF16), vm((640, C), BF16)] + work +
+        [vm((2, 960, KEYS), F32), vm((2, 960, 128), F32)],
+        (nq, lat, comb, bm1, br1, bm0, br0, w_qkv),
+        cost_estimate=pl.CostEstimate(flops=5 * 10 ** 9, transcendentals=0, bytes_accessed=8 * 10 ** 6),
     )
     result = call(
-        main_body,
+        outer_body,
         sds((36, 24, C), BF16),
-        [pltpu.VMEM((1920, C), F32), pltpu.VMEM((1920, C), BF16), pltpu.VMEM((1920, C), BF16),
-         pltpu.VMEM((6, 160, C), F32), pltpu.VMEM((6, 160, C), F32), pltpu.VMEM((16, 256), F32),
-         pltpu.VMEM((36, 24, C), F32), pltpu.VMEM((KEYS, 128), F32), pltpu.VMEM((KEYS, 128), F32),
-         pltpu.VMEM((2, 1920, KEYS), F32),
-         pltpu.VMEM((2, 1920, 128), F32)],
-        (fields, nq, lat, left, right, comb, bm1, br1, bm0, br0, w_qkv, w_proj, w_fc1, w_fc2),
+        [vm((1280, C), F32), vm((1280, C), BF16), vm((1280, C), BF16), vm((6, 160, C), F32), vm((6, 160, C), F32),
+         work[0], vm((36, 24, C), F32)] + work[1:] + [vm((2, 960, KEYS), F32), vm((2, 960, 128), F32)],
+        (fields, nq, lat, left, right, comb, qq, mid, bm1, br1, bm0, br0, w_qkv, w_proj, w_fc1, w_fc2),
     )
     return result.reshape(2, 18, 24, C)
 

time: 46.5 us -> 47 us (1.011)
  starting transfers between devices: 19.2 us -> 14 us
  waiting for transfers between devices: 0.01 us -> 4.93 us
  Pallas kernels: 26.9 us -> 27.7 us
    ppermute x3, starting transfers between devices: 19.2 us -> 14 us  [shift(): lax.ppermute(value, axis, [(s, (s + steps) % count) for s in range(count)])]
    ppermute x3, waiting for transfers between devices: 0.01 us -> 4.93 us  [shift(): lax.ppermute(value, axis, [(s, (s + steps) % count) for s in range(count)])]
    pallas_call x5 -> x8, Pallas kernels: 26.9 us -> 27.7 us  [call(): pl.pallas_call(body, out_shape=outs, scratch_shapes=scratch, compiler_par...]
  transfers between devices with their start and end apart: 3 -> 3, of which waited for: 0 -> 1; matrix products, arithmetic and copies ran while one was open for 0% -> 0% of each run, Pallas kernels for 25% -> 16%
where the time goes in v3:
time: 47 us; the launch traced here: 46.8 us
  Pallas kernels  27.7 us (59%)
  starting transfers between devices  14 us (30%)
  waiting for transfers between devices  4.93 us (10%)
    pallas_call x8, Pallas kernels, call(): pl.pallas_call(body, out_shape=outs, scratch_shapes=scratch, compiler_par...  27.7 us
    ppermute x3, starting transfers between devices, shift(): lax.ppermute(value, axis, [(s, (s + steps) % count) for s in range(count)])  14 us
    ppermute x3, waiting for transfers between devices, shift(): lax.ppermute(value, axis, [(s, (s + steps) % count) for s in range(count)])  4.93 us
  transfers between devices with their start and end apart: 3, of which 1 were waited for; matrix products, arithmetic and copies ran while one was open for 0% of the time, Pallas kernels for 16%

profile of v3, /device:TPU:1, one launch (start us, length us, event | category | flops | bytes accessed | tf_op | source)
XLA Modules:
  0.0 46.8 jit_solution(10026897440527528061)
XLA Ops:
  0.0 2.1 %shard_map.127 = (bf16[6,160,384]{2,1,0:T(8,128)(2,1)S(1)}, f32[8,512]{1,0:T(8,128)S(1)}, bf16[544,384]{1,0:T(8,128)(2,1)S(1)}, f32[13,16,256]{2,1,0:T(8,128)S(1)}) custom-call(bf16[36,24,384]{2,1,0:T(8,128)(2,1)} %bitcast.4, s32[18,2,24]{2,1,0:T(2,128)} %bitcast.8, bf16[3,12,3312]{2,1,0:T(8,128)(2,1)} %bitcast.6), custom_call_target="tpu_custom_call" | custom-call | tf_op jit(solution)/shard_map/pallas_call | solution.py:409
  2.1 8.7 %collective-permute-start = (bf16[544,384]{1,0:T(8,128)(2,1)S(1)}, bf16[544,384]{1,0:T(8,128)(2,1)S(1)}, u32[]{:S(2)}, u32[]{:S(2)}) collective-permute-start(bf16[544,384]{1,0:T(8,128)(2,1)S(1)} %get-tuple-element.25), channel_id=1, source_target_pairs={{0,64},{64,0},{1,65},{65,1},{2,66},{66,2},{3,67},{67,3},{4,68},{68... | collective-permute-start | bytes 1253384 | tf_op jit(solution)/shard_map/ppermute | solution.py:424
  10.9 2.1 %shard_map.129 = (f32[144,128]{1,0:T(8,128)S(1)}, f32[144,128]{1,0:T(8,128)S(1)}, f32[32,256]{1,0:T(8,128)S(1)}, f32[32,256]{1,0:T(8,128)S(1)}, f32[13,24,256]{2,1,0:T(8,128)S(1)}) custom-call(s32[144,144]{1,0:T(8,128)} %index_hbm.1, bf16[3,12,3312]{2,1,0:T(8,128)(2,1)} %bitcast.7, bf16[144,144]{1,0:T(8,128)(2,1)} %constant.10.clone.refs_0_, ...), custom_call_target="tpu_custom_call" | custom-call | flops 1000000000 | bytes 1000000 | tf_op jit(solution)/shard_map/pallas_call | solution.py:409
  13.0 0.0 collective-permute-done.lat.refs_6_
  13.0 8.7 %shard_map.130 = (f32[3200,128]{1,0:T(8,128)S(1)}, f32[3200,128]{1,0:T(8,128)S(1)}, f32[3200,128]{1,0:T(8,128)S(1)}, f32[3200,128]{1,0:T(8,128)S(1)}) custom-call(f32[144,128]{1,0:T(8,128)S(1)} %get-tuple-element.27.refs_0_, f32[144,128]{1,0:T(8,128)S(1)} %get-tuple-element.28.refs_1_, f32[32,256]{1,0:T(8,128)S(1)} %get-tuple-element.29.refs_2_, ...), custom_call_target="tpu_custom_call" | custom-call | flops 10000000000 | bytes 8000000 | tf_op jit(solution)/shard_map/pallas_call | solution.py:409
  21.7 1.9 %collective-permute-start.2 = (bf16[320,384]{1,0:T(8,128)(2,1)S(1)}, bf16[320,384]{1,0:T(8,128)(2,1)S(1)}, u32[]{:S(2)}, u32[]{:S(2)}) collective-permute-start(bf16[320,384]{1,0:T(8,128)(2,1)S(1)} %shard_map.131), channel_id=1, source_target_pairs={{0,63},{1,0},{2,1},{3,2},{4,3},{5,4},{6,5},{7,6},{8,7},{9,8},{10,9... | collective-permute-start | bytes 737288 | tf_op jit(solution)/shard_map/ppermute | solution.py:424
  23.7 3.4 %collective-permute-start.1 = (bf16[336,384]{1,0:T(8,128)(2,1)S(1)}, bf16[336,384]{1,0:T(8,128)(2,1)S(1)}, u32[]{:S(2)}, u32[]{:S(2)}) collective-permute-start(bf16[336,384]{1,0:T(8,128)(2,1)S(1)} %shard_map.128), channel_id=1, source_target_pairs={{0,1},{1,2},{2,3},{3,4},{4,5},{5,6},{6,7},{7,8},{8,9},{9,10},{10,1... | collective-permute-start | bytes 774152 | tf_op jit(solution)/shard_map/ppermute | solution.py:424
  27.0 0.0 copy-start.3
  27.0 1.3 %shard_map.132 = (f32[3200,128]{1,0:T(8,128)S(1)}, f32[3200,128]{1,0:T(8,128)S(1)}, f32[3200,128]{1,0:T(8,128)S(1)}, f32[3200,128]{1,0:T(8,128)S(1)}) custom-call(f32[144,128]{1,0:T(8,128)S(1)} %get-tuple-element.27.refs_0_, f32[144,128]{1,0:T(8,128)S(1)} %get-tuple-element.28.refs_1_, ...), custom_call_target="tpu_custom_call", output_to_operand_aliasing={{0}: (7, {}), {1}: (8, {}), {2}: (9, {}), {3}: (10, {})} | custom-call | flops 10000000000 | bytes 8000000 | tf_op jit(solution)/shard_map/pallas_call | solution.py:409
  28.3 0.0 copy-done.3
  28.3 0.0 copy-start
  28.4 0.0 copy-start.1
  28.4 0.0 copy-start.2
  28.4 0.0 copy-start.4
  28.4 4.2 %shard_map.133 = (f32[6,160,384]{2,1,0:T(8,128)S(1)}, f32[6,80,384]{2,1,0:T(8,128)S(1)}) custom-call(bf16[6,160,384]{2,1,0:T(8,128)(2,1)S(1)} %get-tuple-element.24.nq, bf16[544,384]{1,0:T(8,128)(2,1)S(1)} %collective-permute-done.lat.refs_6_, f32[8,512]{1,0:T(8,128)S(1)} %get-tuple-element.26.comb, f32[3200,128]{1,0:T(8,128)S(1)} %get-tuple-element.37.bm1, ...), custom_call_target="tpu_custom_call" | custom-call | flops 5000000000 | bytes 8000000 | tf_op jit(solution)/shard_map/pallas_call | solution.py:409
  32.6 0.0 collective-permute-done.2.right
  32.6 4.9 %collective-permute-done.1.left = bf16[336,384]{1,0:T(8,128)(2,1)S(1)} collective-permute-done((bf16[336,384]{1,0:T(8,128)(2,1)S(1)}, bf16[336,384]{1,0:T(8,128)(2,1)S(1)}, u32[]{:S(2)}, u32[]{:S(2)}) %collective-permute-start.1) | collective-permute-done | bytes 258080 | tf_op jit(solution)/shard_map/ppermute | solution.py:424
  37.5 0.0 copy-done
  37.5 0.0 copy-done.1
  37.5 0.0 copy-done.2
  37.5 0.0 copy-done.4
  37.6 9.3 %shard_map.134 = bf16[36,24,384]{2,1,0:T(8,128)(2,1)} custom-call(bf16[36,24,384]{2,1,0:T(8,128)(2,1)S(1)} %bitcast.5, bf16[6,160,384]{2,1,0:T(8,128)(2,1)S(1)} %get-tuple-element.24.nq, bf16[544,384]{1,0:T(8,128)(2,1)S(1)} %collective-permute-done.lat.refs_6_, bf16[336,384]{1,0:T(8,128)(2,1)S(1)} %collective-permute-done.1.left, ...), custom_call_target="tpu_custom_call" | custom-call | tf_op jit(solution)/shard_map/pallas_call | solution.py:409
  (2 shorter events, 0.1 us)
Async XLA Ops:
  2.1 10.9 %collective-permute-start = (bf16[544,384]{1,0:T(8,128)(2,1)S(1)}, bf16[544,384]{1,0:T(8,128)(2,1)S(1)}, u32[]{:S(2)}, u32[]{:S(2)}) collective-permute-start(bf16[544,384]{1,0:T(8,128)(2,1)S(1)} %get-tuple-element.25), channel_id=1, source_target_pairs={{0,64},{64,0},{1,65},{65,1},{2,66},{66,2},{3,67},{67,3},{4,68},{68... | collective-permute-start | bytes 1253384 | tf_op jit(solution)/shard_map/ppermute | solution.py:424
  21.7 10.9 %collective-permute-start.2 = (bf16[320,384]{1,0:T(8,128)(2,1)S(1)}, bf16[320,384]{1,0:T(8,128)(2,1)S(1)}, u32[]{:S(2)}, u32[]{:S(2)}) collective-permute-start(bf16[320,384]{1,0:T(8,128)(2,1)S(1)} %shard_map.131), channel_id=1, source_target_pairs={{0,63},{1,0},{2,1},{3,2},{4,3},{5,4},{6,5},{7,6},{8,7},{9,8},{10,9... | collective-permute-start | bytes 737288 | tf_op jit(solution)/shard_map/ppermute | solution.py:424
  23.7 13.9 %collective-permute-start.1 = (bf16[336,384]{1,0:T(8,128)(2,1)S(1)}, bf16[336,384]{1,0:T(8,128)(2,1)S(1)}, u32[]{:S(2)}, u32[]{:S(2)}) collective-permute-start(bf16[336,384]{1,0:T(8,128)(2,1)S(1)} %shard_map.128), channel_id=1, source_target_pairs={{0,1},{1,2},{2,3},{3,4},{4,5},{5,6},{6,7},{7,8},{8,9},{9,10},{10,1... | collective-permute-start | bytes 774152 | tf_op jit(solution)/shard_map/ppermute | solution.py:424
  27.0 1.3 %copy-start.3 = (bf16[384,1152]{1,0:T(8,128)(2,1)S(1)}, bf16[384,1152]{1,0:T(8,128)(2,1)}, u32[]{:S(2)}) copy-start(bf16[384,1152]{1,0:T(8,128)(2,1)} %w_qkv.3) | copy-start | bytes 2654212
  28.3 9.2 %copy-start = (bf16[2,18,24,384]{3,2,1,0:T(8,128)(2,1)S(1)}, bf16[2,18,24,384]{3,2,1,0:T(8,128)(2,1)}, u32[]{:S(2)}) copy-start(bf16[2,18,24,384]{3,2,1,0:T(8,128)(2,1)} %param.13) | copy-start | bytes 1990660
  28.4 9.2 %copy-start.1 = (bf16[384,1536]{1,0:T(8,128)(2,1)S(1)}, bf16[384,1536]{1,0:T(8,128)(2,1)}, u32[]{:S(2)}) copy-start(bf16[384,1536]{1,0:T(8,128)(2,1)} %w_fc1.1) | copy-start | bytes 3538948
  28.4 9.2 %copy-start.2 = (bf16[1536,384]{1,0:T(8,128)(2,1)S(1)}, bf16[1536,384]{1,0:T(8,128)(2,1)}, u32[]{:S(2)}) copy-start(bf16[1536,384]{1,0:T(8,128)(2,1)} %w_fc2.1) | copy-start | bytes 3538948
  28.4 9.2 %copy-start.4 = (bf16[384,384]{1,0:T(8,128)(2,1)S(1)}, bf16[384,384]{1,0:T(8,128)(2,1)}, u32[]{:S(2)}) copy-start(bf16[384,384]{1,0:T(8,128)(2,1)} %w_proj.1) | copy-start | bytes 884740

commit v4 on v3

--- a/solution.py
+++ b/solution.py
@@ -12,7 +12,7 @@
 LOG2E = 1.4426950408889634
 C = 384
 HEADS = 12
-KEYS = 160
+KEYS = 144
 POSITIONS = 3312
 CHUNKS = 13
 ROWS = 40
@@ -27,10 +27,10 @@
     lane = lax.broadcasted_iota(jnp.int32, (1, 512), 1).astype(F32)
     w = floor_div(lane, 256)
     p = lane - 256 * w
-    r2 = floor_div(p, 80)
-    c2 = floor_div(p - 80 * r2, 40)
-    kk = p - 80 * r2 - 40 * c2
-    valid = (p < 160) & (kk < 36)
+    r2 = floor_div(p, 72)
+    c2 = floor_div(p - 72 * r2, 36)
+    kk = p - 72 * r2 - 36 * c2
+    valid = p < 144
     level = floor_div(kk, 18)
     r3 = floor_div(kk - 18 * level, 6)
     src = jnp.where(valid, 12 * w + 6 * c2 + kk - 18 * level - 6 * r3, -1.0)
@@ -53,7 +53,7 @@
     return got
 
 
-def window_order(padded):
+def window_order():
     spots = []
     for r2 in range(2):
         for c2 in range(2):
@@ -61,19 +61,16 @@
                 for r3 in range(3):
                     for c6 in range(6):
                         spots.append(level * 72 + (r2 * 3 + r3) * 12 + c2 * 6 + c6)
-            if padded:
-                spots += [-1] * 4
     return np.array(spots)
 
 
 def index_constants():
-    pick = (window_order(False)[:, None] == np.arange(144)[None]).astype(np.float32)
-    place = (np.arange(144)[:, None] == window_order(True)[None]).astype(np.float32)
-    tile = (np.arange(32)[:, None] == (np.arange(256) % 32)[None]).astype(np.float32)
-    keep = ((np.arange(144) % 8)[:, None] == (np.arange(256) // 32)[None]).astype(np.float32)
+    pick = (window_order()[:, None] == np.arange(144)[None]).astype(np.float32)
+    tile = (np.arange(16)[:, None] == (np.arange(256) % 16)[None]).astype(np.float32)
     row = np.arange(144)
-    gather = ((16 * (row // 72) + row % 72 // 8)[None] == np.arange(32)[:, None]).astype(np.float32)
-    return pick, place, tile, keep, gather
+    keep = ((row % 72 % 16)[:, None] == (np.arange(256) // 16)[None]).astype(np.float32)
+    gather = ((8 * (row // 72) + row % 72 // 16)[None] == np.arange(16)[:, None]).astype(np.float32)
+    return pick, pick.T, tile, keep, gather
 
 
 def dot(a, b):
@@ -162,7 +159,7 @@
         picked = dot(pick[...], part.astype(F32).astype(BF16)).astype(BF16)
         full = dot(picked, place[...])
         m_ref[...] = full[:, 0:128]
-        wide = dot(full[:, 128:160].astype(BF16), tile[...]) * keep[...]
+        wide = dot(full[:, 128:144].astype(BF16), tile[...]) * keep[...]
         r_ref[...] = dot(gather[...], wide.astype(BF16))
     copies[6].wait()
     for c in range(CHUNKS):
@@ -171,7 +168,9 @@
 
 
 def early_blocks():
-    return jnp.maximum(7 - lax.axis_index("lon") % 32, 0)
+    lon = lax.axis_index("lon")
+    late = (lon == 0) & (lax.axis_index("ens") == 0)
+    return jnp.where(late, 2, jnp.maximum(7 - lon % 32, 0))
 
 
 def bias_body(late, lo_m, hi_m, lo_r, hi_r, own, inner, swap, *refs):
@@ -217,14 +216,14 @@
 
         @pl.when(done < 4 if late else done >= 4)
         def _():
-            for g in range(9):
-                out = look(table, lo_r[16 * half + g:16 * half + g + 1, :], hi_r[16 * half + g:16 * half + g + 1, :])
-                for q in range(8):
-                    i = 8 * g + q
+            for g in range(5):
+                out = look(table, lo_r[8 * half + g:8 * half + g + 1, :], hi_r[8 * half + g:8 * half + g + 1, :])
+                for q in range(min(16, 72 - 16 * g)):
+                    i = 16 * g + q
                     spot = i + 4 * (i // 36)
-                    piece = out[:, 128 * (q // 4):128 * (q // 4) + 128]
-                    if q % 4:
-                        piece = pltpu.roll(piece, 128 - 32 * (q % 4), axis=1)
+                    piece = out[:, 128 * (q // 8):128 * (q // 8) + 128]
+                    if q % 8:
+                        piece = pltpu.roll(piece, 128 - 16 * (q % 8), axis=1)
                     rem[pl.ds(spot, ROWS, stride=SPAN), :] = piece
 
 
@@ -238,16 +237,16 @@
 
 
 def put(xs, group, rt, second, block):
-    at = 640 * group + 80 * rt + 40 * second
-    xs[at:at + block.shape[0], :] = block
+    at = 576 * group + 72 * rt + 36 * second
+    xs[at:at + 36, :] = block[0:36, :]
 
 
 def key_values(xs, kk, vv, w_qkv, count):
     def project(step, carry):
-        at = pl.multiple_of(step * 320, 320)
-        y = dot(xs[pl.ds(at, 320), :].astype(BF16), w_qkv[:, C:3 * C])
-        kk[pl.ds(at, 320), :] = y[:, 0:C].astype(BF16)
-        vv[pl.ds(at, 320), :] = y[:, C:2 * C].astype(BF16)
+        at = pl.multiple_of(step * 288, 288)
+        y = dot(xs[pl.ds(at, 288), :].astype(BF16), w_qkv[:, C:3 * C])
+        kk[pl.ds(at, 288), :] = y[:, 0:C].astype(BF16)
+        vv[pl.ds(at, 288), :] = y[:, C:2 * C].astype(BF16)
         return carry
 
     lax.fori_loop(0, count, project, 0, unroll=count)
@@ -261,7 +260,9 @@
         jnp.concatenate([hot, jnp.zeros((64, KEYS), F32)], axis=0).astype(BF16),
         jnp.concatenate([jnp.where(eye, 1.0, 0.0), jnp.zeros((64, 128), F32)], axis=0).astype(BF16),
         (((0,), (0,)), ((), ())), preferred_element_type=F32)
-    qf[...] = seen
+    qf[...] = jnp.zeros((160, 128), F32)
+    for n in range(4):
+        qf[40 * n:40 * n + 36, :] = seen[36 * n:36 * n + 36, :]
     kf[...] = (seen - 1.0) * 1e30
 
 
@@ -286,14 +287,14 @@
             near = qf[80 * r2 + c0:80 * r2 + c0 + nrow, :]
             for g in range(3):
                 sl = slice(128 * g, 128 * g + 128)
-                k = jnp.concatenate([kk[pl.ds(pl.multiple_of(640 * n + 160 * t, 160), KEYS), sl], far], axis=1)
+                k = jnp.concatenate([kk[pl.ds(pl.multiple_of(576 * n + 144 * t, 144), KEYS), sl], far], axis=1)
                 q = qq[rt - 1, q0:q0 + nrow, sl]
                 qs = jnp.concatenate([jnp.concatenate([jnp.where(m, q, 0.0), near], axis=1) for m in heads],
                                      axis=0).astype(BF16)
                 s = lax.dot_general(qs, k, (((1,), (1,)), ((), ())), preferred_element_type=F32)
                 for h in range(4):
                     th = pl.multiple_of((th0 + 4 * g + h) * SPAN, SPAN) + c0
-                    b = jnp.concatenate([bm[pl.ds(th, nrow), :], br[pl.ds(th, nrow), :][:, 0:32]], axis=1)
+                    b = jnp.concatenate([bm[pl.ds(th, nrow), :], br[pl.ds(th, nrow), :][:, 0:16]], axis=1)
                     x = s[h * nrow:(h + 1) * nrow, :] * SCALE + b
                     sc[r2, top:top + nrow, :] = x
                     mx[r2, top:top + nrow, :] = jnp.broadcast_to(jnp.max(x, axis=1, keepdims=True), (nrow, 128))
@@ -309,10 +310,10 @@
                 parts = []
                 for _ in range(4):
                     m = mx[r2, top:top + nrow, :]
-                    x = sc[r2, top:top + nrow, :] - jnp.concatenate([m, m[:, 0:32]], axis=1)
+                    x = sc[r2, top:top + nrow, :] - jnp.concatenate([m, m[:, 0:16]], axis=1)
                     parts.append(jnp.exp2(x).astype(BF16))
                     top += nrow
-                v = vv[pl.ds(pl.multiple_of(640 * n + 160 * t, 160), KEYS), sl]
+                v = vv[pl.ds(pl.multiple_of(576 * n + 144 * t, 144), KEYS), sl]
                 o = dot(jnp.concatenate(parts, axis=0), jnp.concatenate([v, ones], axis=1))
                 os = [o[h * nrow:(h + 1) * nrow, :] for h in range(4)]
                 num, den = os[3][:, 0:128], os[3][:, 128:256]
@@ -334,10 +335,11 @@
 
 
 def inner_body(nq, lat, comb, bm1, br1, bm0, br0, w_qkv, qq, ctx, xs, kk, vv, rows, qf, kf, sc, mx):
-    xs[0:80, :] = lat[200:280, :].astype(F32)
-    xs[560:640, :] = lat[0:160, :].astype(F32)[40:120, :]
-    for rt in range(6):
-        xs[80 * rt + 80:80 * rt + 160, :] = nq[rt].astype(F32)[40:120, :]
+    for rt in range(8):
+        block = lat[160:320, :] if rt == 0 else lat[0:160, :] if rt == 7 else nq[rt - 1]
+        block = block.astype(F32)
+        put(xs, 0, rt, 0, block[40:80, :])
+        put(xs, 0, rt, 1, block[80:120, :])
     key_values(xs, kk, vv, w_qkv, 2)
     for rt in range(6):
         qq[rt] = dot(nq[rt], w_qkv[:, 0:C]).astype(BF16).astype(F32)
@@ -446,7 +448,7 @@
     consts = tuple(jnp.asarray(c, k) for c, k in zip(index_constants(), kinds))
     *found, inner = call(
         index_body,
-        (sds((144, 128), F32), sds((144, 128), F32), sds((32, 256), F32), sds((32, 256), F32),
+        (sds((144, 128), F32), sds((144, 128), F32), sds((16, 256), F32), sds((16, 256), F32),
          sds((CHUNKS, 24, 256), F32)),
         [pltpu.VMEM((144, 144), jnp.int32), pltpu.VMEM((2, HEADS, POSITIONS), BF16)] +
         [pltpu.VMEM(c.shape, c.dtype) for c in consts] + [pltpu.SemaphoreType.DMA((7,))],
@@ -479,11 +481,11 @@
     right = shift(pay_l, "lon", -1)
     bm0, br0, bm1, br1 = bias(True, tuple(some))
     vm = pltpu.VMEM
-    work = [vm((8, 256), F32), vm((KEYS, 128), F32), vm((KEYS, 128), F32)]
+    work = [vm((8, 256), F32), vm((160, 128), F32), vm((KEYS, 128), F32)]
     qq, mid = call(
         inner_body,
         (sds((6, 160, C), F32), sds((6, SPAN, C), F32)),
-        [vm((640, C), F32), vm((640, C), BF16), vm((640, C), BF16)] + work +
+        [vm((576, C), F32), vm((576, C), BF16), vm((576, C), BF16)] + work +
         [vm((2, 960, KEYS), F32), vm((2, 960, 128), F32)],
         (nq, lat, comb, bm1, br1, bm0, br0, w_qkv),
         cost_estimate=pl.CostEstimate(flops=5 * 10 ** 9, transcendentals=0, bytes_accessed=8 * 10 ** 6),
@@ -491,7 +493,7 @@
     result = call(
         outer_body,
         sds((36, 24, C), BF16),
-        [vm((1280, C), F32), vm((1280, C), BF16), vm((1280, C), BF16), vm((6, 160, C), F32), vm((6, 160, C), F32),
+        [vm((1152, C), F32), vm((1152, C), BF16), vm((1152, C), BF16), vm((6, 160, C), F32), vm((6, 160, C), F32),
          work[0], vm((36, 24, C), F32)] + work[1:] + [vm((2, 960, KEYS), F32), vm((2, 960, 128), F32)],
         (fields, nq, lat, left, right, comb, qq, mid, bm1, br1, bm0, br0, w_qkv, w_proj, w_fc1, w_fc2),
     )

time: 47 us -> 44.7 us (0.951)
  waiting for transfers between devices: 4.93 us -> 0.57 us
  starting transfers between devices: 14 us -> 16.7 us
  Pallas kernels: 27.7 us -> 27 us
    ppermute x3, waiting for transfers between devices: 4.93 us -> 0.57 us  [shift(): lax.ppermute(value, axis, [(s, (s + steps) % count) for s in range(count)])]
    ppermute x3, starting transfers between devices: 14 us -> 16.7 us  [shift(): lax.ppermute(value, axis, [(s, (s + steps) % count) for s in range(count)])]
    pallas_call x8, Pallas kernels: 27.7 us -> 27 us  [call(): pl.pallas_call(body, out_shape=outs, scratch_shapes=scratch, compiler_par...]
  transfers between devices with their start and end apart: 3 -> 3, of which waited for: 1 -> 1; matrix products, arithmetic and copies ran while one was open for 0% -> 0% of each run, Pallas kernels for 16% -> 30%
where the time goes in v4:
time: 44.7 us; the launch traced here: 44.4 us
  Pallas kernels  27 us (60%)
  starting transfers between devices  16.7 us (37%)
  waiting for transfers between devices  0.57 us (1%)
    pallas_call x8, Pallas kernels, call(): pl.pallas_call(body, out_shape=outs, scratch_shapes=scratch, compiler_par...  27 us
    ppermute x3, starting transfers between devices, shift(): lax.ppermute(value, axis, [(s, (s + steps) % count) for s in range(count)])  16.7 us
  transfers between devices with their start and end apart: 3, of which 1 were waited for; matrix products, arithmetic and copies ran while one was open for 0% of the time, Pallas kernels for 30%

profile of v4, /device:TPU:1, one launch (start us, length us, event | category | flops | bytes accessed | tf_op | source)
XLA Modules:
  0.0 44.4 jit_solution(1625661493697704184)
XLA Ops:
  0.0 2.1 %shard_map.127 = (bf16[6,160,384]{2,1,0:T(8,128)(2,1)S(1)}, f32[8,512]{1,0:T(8,128)S(1)}, bf16[544,384]{1,0:T(8,128)(2,1)S(1)}, f32[13,16,256]{2,1,0:T(8,128)S(1)}) custom-call(bf16[36,24,384]{2,1,0:T(8,128)(2,1)} %bitcast.4, s32[18,2,24]{2,1,0:T(2,128)} %bitcast.8, bf16[3,12,3312]{2,1,0:T(8,128)(2,1)} %bitcast.6), custom_call_target="tpu_custom_call" | custom-call | tf_op jit(solution)/shard_map/pallas_call | solution.py:411
  2.1 8.7 %collective-permute-start = (bf16[544,384]{1,0:T(8,128)(2,1)S(1)}, bf16[544,384]{1,0:T(8,128)(2,1)S(1)}, u32[]{:S(2)}, u32[]{:S(2)}) collective-permute-start(bf16[544,384]{1,0:T(8,128)(2,1)S(1)} %get-tuple-element.25), channel_id=1, source_target_pairs={{0,64},{64,0},{1,65},{65,1},{2,66},{66,2},{3,67},{67,3},{4,68},{68... | collective-permute-start | bytes 1253384 | tf_op jit(solution)/shard_map/ppermute | solution.py:426
  10.9 2.1 %shard_map.129 = (f32[144,128]{1,0:T(8,128)S(1)}, f32[144,128]{1,0:T(8,128)S(1)}, f32[16,256]{1,0:T(8,128)S(1)}, f32[16,256]{1,0:T(8,128)S(1)}, f32[13,24,256]{2,1,0:T(8,128)S(1)}) custom-call(s32[144,144]{1,0:T(8,128)} %index_hbm.1, bf16[3,12,3312]{2,1,0:T(8,128)(2,1)} %bitcast.7, bf16[144,144]{1,0:T(8,128)(2,1)} %constant.10.clone.refs_0_, ...), custom_call_target="tpu_custom_call" | custom-call | flops 1000000000 | bytes 1000000 | tf_op jit(solution)/shard_map/pallas_call | solution.py:411
  13.0 0.0 collective-permute-done.lat.refs_6_
  13.0 2.6 %shard_map.130 = (f32[3200,128]{1,0:T(8,128)S(1)}, f32[3200,128]{1,0:T(8,128)S(1)}, f32[3200,128]{1,0:T(8,128)S(1)}, f32[3200,128]{1,0:T(8,128)S(1)}) custom-call(f32[144,128]{1,0:T(8,128)S(1)} %get-tuple-element.27.refs_0_, f32[144,128]{1,0:T(8,128)S(1)} %get-tuple-element.28.refs_1_, f32[16,256]{1,0:T(8,128)S(1)} %get-tuple-element.29.refs_2_, ...), custom_call_target="tpu_custom_call" | custom-call | flops 10000000000 | bytes 8000000 | tf_op jit(solution)/shard_map/pallas_call | solution.py:411
  15.6 6.0 %collective-permute-start.2 = (bf16[320,384]{1,0:T(8,128)(2,1)S(1)}, bf16[320,384]{1,0:T(8,128)(2,1)S(1)}, u32[]{:S(2)}, u32[]{:S(2)}) collective-permute-start(bf16[320,384]{1,0:T(8,128)(2,1)S(1)} %shard_map.131), channel_id=1, source_target_pairs={{0,63},{1,0},{2,1},{3,2},{4,3},{5,4},{6,5},{7,6},{8,7},{9,8},{10,9... | collective-permute-start | bytes 737288 | tf_op jit(solution)/shard_map/ppermute | solution.py:426
  21.7 1.9 %collective-permute-start.1 = (bf16[336,384]{1,0:T(8,128)(2,1)S(1)}, bf16[336,384]{1,0:T(8,128)(2,1)S(1)}, u32[]{:S(2)}, u32[]{:S(2)}) collective-permute-start(bf16[336,384]{1,0:T(8,128)(2,1)S(1)} %shard_map.128), channel_id=1, source_target_pairs={{0,1},{1,2},{2,3},{3,4},{4,5},{5,6},{6,7},{7,8},{8,9},{9,10},{10,1... | collective-permute-start | bytes 774152 | tf_op jit(solution)/shard_map/ppermute | solution.py:426
  23.6 0.0 copy-start.3
  23.6 6.9 %shard_map.132 = (f32[3200,128]{1,0:T(8,128)S(1)}, f32[3200,128]{1,0:T(8,128)S(1)}, f32[3200,128]{1,0:T(8,128)S(1)}, f32[3200,128]{1,0:T(8,128)S(1)}) custom-call(f32[144,128]{1,0:T(8,128)S(1)} %get-tuple-element.27.refs_0_, f32[144,128]{1,0:T(8,128)S(1)} %get-tuple-element.28.refs_1_, ...), custom_call_target="tpu_custom_call", output_to_operand_aliasing={{0}: (7, {}), {1}: (8, {}), {2}: (9, {}), {3}: (10, {})} | custom-call | flops 10000000000 | bytes 8000000 | tf_op jit(solution)/shard_map/pallas_call | solution.py:411
  30.5 0.0 copy-done.3
  30.5 0.0 copy-start
  30.5 0.0 copy-start.1
  30.5 0.0 copy-start.2
  30.5 0.0 copy-start.4
  30.6 4.1 %shard_map.133 = (f32[6,160,384]{2,1,0:T(8,128)S(1)}, f32[6,80,384]{2,1,0:T(8,128)S(1)}) custom-call(bf16[6,160,384]{2,1,0:T(8,128)(2,1)S(1)} %get-tuple-element.24.nq, bf16[544,384]{1,0:T(8,128)(2,1)S(1)} %collective-permute-done.lat.refs_6_, f32[8,512]{1,0:T(8,128)S(1)} %get-tuple-element.26.comb, f32[3200,128]{1,0:T(8,128)S(1)} %get-tuple-element.37.bm1, ...), custom_call_target="tpu_custom_call" | custom-call | flops 5000000000 | bytes 8000000 | tf_op jit(solution)/shard_map/pallas_call | solution.py:411
  34.7 0.0 collective-permute-done.2.right
  34.7 0.6 %collective-permute-done.1.left = bf16[336,384]{1,0:T(8,128)(2,1)S(1)} collective-permute-done((bf16[336,384]{1,0:T(8,128)(2,1)S(1)}, bf16[336,384]{1,0:T(8,128)(2,1)S(1)}, u32[]{:S(2)}, u32[]{:S(2)}) %collective-permute-start.1) | collective-permute-done | bytes 258080 | tf_op jit(solution)/shard_map/ppermute | solution.py:426
  35.3 0.0 copy-done
  35.3 0.0 copy-done.1
  35.3 0.0 copy-done.2
  35.3 0.0 copy-done.4
  35.3 9.1 %shard_map.134 = bf16[36,24,384]{2,1,0:T(8,128)(2,1)} custom-call(bf16[36,24,384]{2,1,0:T(8,128)(2,1)S(1)} %bitcast.5, bf16[6,160,384]{2,1,0:T(8,128)(2,1)S(1)} %get-tuple-element.24.nq, bf16[544,384]{1,0:T(8,128)(2,1)S(1)} %collective-permute-done.lat.refs_6_, bf16[336,384]{1,0:T(8,128)(2,1)S(1)} %collective-permute-done.1.left, ...), custom_call_target="tpu_custom_call" | custom-call | tf_op jit(solution)/shard_map/pallas_call | solution.py:411
  (2 shorter events, 0.1 us)
Async XLA Ops:
  2.1 10.9 %collective-permute-start = (bf16[544,384]{1,0:T(8,128)(2,1)S(1)}, bf16[544,384]{1,0:T(8,128)(2,1)S(1)}, u32[]{:S(2)}, u32[]{:S(2)}) collective-permute-start(bf16[544,384]{1,0:T(8,128)(2,1)S(1)} %get-tuple-element.25), channel_id=1, source_target_pairs={{0,64},{64,0},{1,65},{65,1},{2,66},{66,2},{3,67},{67,3},{4,68},{68... | collective-permute-start | bytes 1253384 | tf_op jit(solution)/shard_map/ppermute | solution.py:426
  15.6 19.1 %collective-permute-start.2 = (bf16[320,384]{1,0:T(8,128)(2,1)S(1)}, bf16[320,384]{1,0:T(8,128)(2,1)S(1)}, u32[]{:S(2)}, u32[]{:S(2)}) collective-permute-start(bf16[320,384]{1,0:T(8,128)(2,1)S(1)} %shard_map.131), channel_id=1, source_target_pairs={{0,63},{1,0},{2,1},{3,2},{4,3},{5,4},{6,5},{7,6},{8,7},{9,8},{10,9... | collective-permute-start | bytes 737288 | tf_op jit(solution)/shard_map/ppermute | solution.py:426
  21.7 13.6 %collective-permute-start.1 = (bf16[336,384]{1,0:T(8,128)(2,1)S(1)}, bf16[336,384]{1,0:T(8,128)(2,1)S(1)}, u32[]{:S(2)}, u32[]{:S(2)}) collective-permute-start(bf16[336,384]{1,0:T(8,128)(2,1)S(1)} %shard_map.128), channel_id=1, source_target_pairs={{0,1},{1,2},{2,3},{3,4},{4,5},{5,6},{6,7},{7,8},{8,9},{9,10},{10,1... | collective-permute-start | bytes 774152 | tf_op jit(solution)/shard_map/ppermute | solution.py:426
  23.6 6.9 %copy-start.3 = (bf16[384,1152]{1,0:T(8,128)(2,1)S(1)}, bf16[384,1152]{1,0:T(8,128)(2,1)}, u32[]{:S(2)}) copy-start(bf16[384,1152]{1,0:T(8,128)(2,1)} %w_qkv.3) | copy-start | bytes 2654212
  30.5 4.8 %copy-start = (bf16[2,18,24,384]{3,2,1,0:T(8,128)(2,1)S(1)}, bf16[2,18,24,384]{3,2,1,0:T(8,128)(2,1)}, u32[]{:S(2)}) copy-start(bf16[2,18,24,384]{3,2,1,0:T(8,128)(2,1)} %param.13) | copy-start | bytes 1990660
  30.5 4.8 %copy-start.1 = (bf16[384,1536]{1,0:T(8,128)(2,1)S(1)}, bf16[384,1536]{1,0:T(8,128)(2,1)}, u32[]{:S(2)}) copy-start(bf16[384,1536]{1,0:T(8,128)(2,1)} %w_fc1.1) | copy-start | bytes 3538948
  30.5 4.8 %copy-start.2 = (bf16[1536,384]{1,0:T(8,128)(2,1)S(1)}, bf16[1536,384]{1,0:T(8,128)(2,1)}, u32[]{:S(2)}) copy-start(bf16[1536,384]{1,0:T(8,128)(2,1)} %w_fc2.1) | copy-start | bytes 3538948
  30.5 4.8 %copy-start.4 = (bf16[384,384]{1,0:T(8,128)(2,1)S(1)}, bf16[384,384]{1,0:T(8,128)(2,1)}, u32[]{:S(2)}) copy-start(bf16[384,384]{1,0:T(8,128)(2,1)} %w_proj.1) | copy-start | bytes 884740

commit v5 on v4

--- a/solution.py
+++ b/solution.py
@@ -91,8 +91,11 @@
     return copies
 
 
-def prep_body(fields_hbm, region_hbm, eb_hbm, nq, comb, pay, own, xq, reg, fields, region, eb, sems):
-    copies = fetch_all(((fields_hbm, fields), (region_hbm, region), (eb_hbm.at[2], eb)), sems)
+def prep_body(fields_hbm, region_hbm, eb_hbm, index_hbm, *refs):
+    consts, (nq, comb, pay, own, lo_m, hi_m, lo_r, hi_r, inner) = refs[:5], refs[5:14]
+    (xq, reg, fields, region, eb, index), bufs, sems = refs[14:20], refs[20:25], refs[25]
+    copies = fetch_all(((fields_hbm, fields), (region_hbm, region), (eb_hbm, eb), (index_hbm, index)) +
+                       tuple(zip(consts, bufs)), sems)
     for cs in range(4):
         for rt in range(6):
             xq[rt, 40 * cs + 32:40 * cs + 40, :] = jnp.zeros((8, C), F32)
@@ -124,34 +127,11 @@
     pay[320:336, 0:256] = last.astype(BF16)
     copies[2].wait()
     for c in range(CHUNKS):
-        own[c] = jnp.concatenate([spread_table(eb, c), jnp.zeros((4, 256), F32)], axis=0)
+        own[c] = jnp.concatenate([spread_table(eb.at[2], c), jnp.zeros((4, 256), F32)], axis=0)
         pay[336 + 16 * c:352 + 16 * c, 0:256] = own[c].astype(BF16)
-
-
-def column(nq, lat, scr, cs):
-    sl = slice(40 * cs, 40 * cs + 40)
-    scr[0:40, :] = lat[160:320, :].astype(F32)[sl, :]
-    scr[280:320, :] = lat[0:160, :].astype(F32)[sl, :]
-    for rt in range(6):
-        scr[40 * rt + 40:40 * rt + 80, :] = nq[rt].astype(F32)[sl, :]
-    return scr[...].astype(BF16)
-
-
-def right_body(nq, lat, comb, pay, scr):
-    pay[0:320, :] = column(nq, lat, scr, 3)
-    top = lat[320:336, 0:256].astype(F32)
-    rows = jnp.concatenate([top[1:2, :], comb[0:3, 256:512], jnp.zeros((12, 256), F32)], axis=0)
-    pay[320:336, 0:256] = rows.astype(BF16)
-
-
-def left_body(nq, lat, after, pay, scr):
-    pay[...] = column(nq, lat, scr, 0)
-
-
-def index_body(index_hbm, eb_hbm, *refs):
-    consts, (lo_m, hi_m, lo_r, hi_r, inner, index, eb), bufs, sems = refs[:5], refs[5:12], refs[12:17], refs[17]
-    copies = fetch_all(((index_hbm, index),) + tuple(zip(consts, bufs)) + ((eb_hbm.at[0:2], eb),), sems)
-    for copy in copies[:6]:
+        inner[c, 0:12, :] = spread_table(eb.at[0], c)
+        inner[c, 12:24, :] = spread_table(eb.at[1], c)
+    for copy in copies[3:]:
         copy.wait()
     pick, place, tile, keep, gather = bufs
     idx = index[...]
@@ -161,22 +141,40 @@
         m_ref[...] = full[:, 0:128]
         wide = dot(full[:, 128:144].astype(BF16), tile[...]) * keep[...]
         r_ref[...] = dot(gather[...], wide.astype(BF16))
-    copies[6].wait()
-    for c in range(CHUNKS):
-        inner[c, 0:12, :] = spread_table(eb.at[0], c)
-        inner[c, 12:24, :] = spread_table(eb.at[1], c)
-
-
-def early_blocks():
+
+
+def column(nq, lat, scr, cs):
+    sl = slice(40 * cs, 40 * cs + 40)
+    scr[0:40, :] = lat[160:320, :].astype(F32)[sl, :]
+    scr[280:320, :] = lat[0:160, :].astype(F32)[sl, :]
+    for rt in range(6):
+        scr[40 * rt + 40:40 * rt + 80, :] = nq[rt].astype(F32)[sl, :]
+    return scr[...].astype(BF16)
+
+
+def right_body(nq, lat, comb, pay, scr):
+    pay[0:320, :] = column(nq, lat, scr, 3)
+    top = lat[320:336, 0:256].astype(F32)
+    rows = jnp.concatenate([top[1:2, :], comb[0:3, 256:512], jnp.zeros((12, 256), F32)], axis=0)
+    pay[320:336, 0:256] = rows.astype(BF16)
+
+
+def left_body(nq, lat, after, pay, scr):
+    pay[...] = column(nq, lat, scr, 0)
+
+
+def block_range(stage):
     lon = lax.axis_index("lon")
-    late = (lon == 0) & (lax.axis_index("ens") == 0)
-    return jnp.where(late, 2, jnp.maximum(7 - lon % 32, 0))
-
-
-def bias_body(late, lo_m, hi_m, lo_r, hi_r, own, inner, swap, *refs):
-    main0, rem0, main1, rem1, tabs = refs[4:] if late else refs
+    first = jnp.where((lon == 0) & (lax.axis_index("lat") == 1) & (lax.axis_index("ens") == 0), 4, 0)
+    second = jnp.maximum(first, 2)
+    third = jnp.maximum(second, 8 - lon % 32)
+    return ((0, first), (first, second), (second, third), (third, 8))[stage]
+
+
+def bias_body(stage, lo_m, hi_m, lo_r, hi_r, own, inner, swap, *refs):
+    main0, rem0, main1, rem1, tabs = (refs[0:4] + refs[-1:]) if stage == 0 else refs[-5:]
+    begin, end = block_range(stage)
     low = lax.broadcasted_iota(jnp.int32, (256, 256), 0).astype(F32)
-    early = early_blocks()
 
     def look(table, lo, hi):
         hot = jnp.where(low == lo, 1.0, 0.0).astype(BF16)
@@ -189,12 +187,11 @@
     for c in range(CHUNKS):
         tabs[ROWS * c + 16:ROWS * c + ROWS, :] = inner[c]
 
-    for half, main, rem in ((0, main0, rem0), (1, main1, rem1)):
+    for half, main, rem in ((0, main0, rem0), (1, main1, rem1))[:1 if stage < 2 else 2]:
         for c in range(CHUNKS):
             tabs[ROWS * c:ROWS * c + 16, :] = \
                 swap[336 + 16 * c:352 + 16 * c, 0:256].astype(F32) if half else own[c]
         table = tabs[...].astype(BF16)
-        done = jnp.clip(early - 4 * half, 0, 4)
 
         def pairs(block, carry):
             first = 24 * block
@@ -209,12 +206,9 @@
                 main[pl.ds(spot + 1, ROWS, stride=SPAN), :] = out[:, 128:256]
             return carry
 
-        if late:
-            lax.fori_loop(jnp.minimum(done, 3), 3, pairs, 0)
-        else:
-            lax.fori_loop(0, jnp.minimum(done, 3), pairs, 0)
-
-        @pl.when(done < 4 if late else done >= 4)
+        lax.fori_loop(jnp.clip(begin - 4 * half, 0, 3), jnp.clip(end - 4 * half, 0, 3), pairs, 0)
+
+        @pl.when((begin <= 4 * half + 3) & (end > 4 * half + 3))
         def _():
             for g in range(5):
                 out = look(table, lo_r[8 * half + g:8 * half + g + 1, :], hi_r[8 * half + g:8 * half + g + 1, :])
@@ -434,43 +428,43 @@
     fields = fields.reshape(36, 24, C)
     region = region_ids.transpose(1, 0, 2)
     tables = earth_bias.transpose(0, 2, 1)
-    nq, comb, pay, own = call(
-        prep_body,
-        (sds((6, 160, C), BF16), sds((8, 512), F32), sds((544, C), BF16), sds((CHUNKS, 16, 256), F32)),
-        [pltpu.VMEM((6, 160, C), F32), pltpu.VMEM((36, 24), F32), pltpu.VMEM((36, 24, C), BF16),
-         pltpu.VMEM((18, 2, 24), jnp.int32), pltpu.VMEM((HEADS, POSITIONS), BF16), pltpu.SemaphoreType.DMA((3,))],
-        tuple(hold(x) for x in (fields, region, tables)),
-        in_specs=[pl.BlockSpec(memory_space=pltpu.HBM)] * 3,
-    )
-    lat = shift(pay, "lat", 1)
-
+    vm = pltpu.VMEM
     kinds = (BF16, BF16, BF16, F32, BF16)
     consts = tuple(jnp.asarray(c, k) for c, k in zip(index_constants(), kinds))
-    *found, inner = call(
-        index_body,
-        (sds((144, 128), F32), sds((144, 128), F32), sds((16, 256), F32), sds((16, 256), F32),
+    nq, comb, pay, own, *found, inner = call(
+        prep_body,
+        (sds((6, 160, C), BF16), sds((8, 512), F32), sds((544, C), BF16), sds((CHUNKS, 16, 256), F32),
+         sds((144, 128), F32), sds((144, 128), F32), sds((16, 256), F32), sds((16, 256), F32),
          sds((CHUNKS, 24, 256), F32)),
-        [pltpu.VMEM((144, 144), jnp.int32), pltpu.VMEM((2, HEADS, POSITIONS), BF16)] +
-        [pltpu.VMEM(c.shape, c.dtype) for c in consts] + [pltpu.SemaphoreType.DMA((7,))],
-        tuple(hold(x) for x in (bias_index, tables) + consts),
-        in_specs=[pl.BlockSpec(memory_space=pltpu.HBM)] * 7,
-        cost_estimate=pl.CostEstimate(flops=10 ** 9, transcendentals=0, bytes_accessed=10 ** 6),
+        [vm((6, 160, C), F32), vm((36, 24), F32), vm((36, 24, C), BF16), vm((18, 2, 24), jnp.int32),
+         vm((3, HEADS, POSITIONS), BF16), vm((144, 144), jnp.int32)] +
+        [vm(c.shape, c.dtype) for c in consts] + [pltpu.SemaphoreType.DMA((9,))],
+        tuple(hold(x) for x in (fields, region, tables, bias_index) + consts),
+        in_specs=[pl.BlockSpec(memory_space=pltpu.HBM)] * 9,
     )
 
-    def bias(late, extra):
+    def bias(stage, extra, kept):
+        count = len(kept)
+        table = (sds((ROWS * SPAN, 128), F32),) * 4
+        alias = {7 + n: n for n in range(4)} if stage else {7: 4}
         return call(
-            lambda *refs: bias_body(late, *refs),
-            (sds((ROWS * SPAN, 128), F32),) * 4,
-            [pltpu.VMEM((CHUNKS * ROWS, 256), F32)],
-            tuple(found) + (own, inner, lat) + extra,
-            cost_estimate=pl.CostEstimate(flops=10 ** 10, transcendentals=0,
+            lambda *refs: bias_body(stage, *refs[:7], *refs[7 + count:]),
+            table if stage else table + (sds(pay.shape, pay.dtype),),
+            [vm((CHUNKS * ROWS, 256), F32)],
+            tuple(found) + (own, inner, extra) + kept,
+            in_specs=[pl.BlockSpec(memory_space=vm)] * 7 + [pl.BlockSpec(memory_space=vm if stage else pl.ANY)] * count,
+            out_specs=tuple([pl.BlockSpec(memory_space=vm)] * 4 + [pl.BlockSpec(memory_space=pl.ANY)] * (not stage)),
+            cost_estimate=pl.CostEstimate(flops=10 ** 10 if stage > 1 else 3 * 10 ** 9, transcendentals=0,
                                           bytes_accessed=8 * 10 ** 6),
-            input_output_aliases={7 + n: n for n in range(4)} if late else {},
+            input_output_aliases=alias,
         )
 
+    *some, pay = bias(0, own, (pay,))
+    lat = shift(pay, "lat", 1)
+    some = bias(1, own, tuple(some))
     pay_r = call(right_body, sds((336, C), BF16), [pltpu.VMEM((320, C), F32)], (nq, lat, comb))
     left = shift(pay_r, "lon", 1)
-    some = bias(False, ())
+    some = bias(2, lat, tuple(some))
     pay_l = call(
         left_body,
         sds((320, C), BF16),
@@ -479,7 +473,7 @@
         in_specs=[pl.BlockSpec(memory_space=pltpu.VMEM)] * 2 + [pl.BlockSpec(memory_space=pl.ANY)],
     )
     right = shift(pay_l, "lon", -1)
-    bm0, br0, bm1, br1 = bias(True, tuple(some))
+    bm0, br0, bm1, br1 = bias(3, lat, tuple(some))
     vm = pltpu.VMEM
     work = [vm((8, 256), F32), vm((160, 128), F32), vm((KEYS, 128), F32)]
     qq, mid = call(

time: 44.7 us -> 46.2 us (1.034)
  waiting for transfers between devices: 0.57 us -> 7.66 us
  starting transfers between devices: 16.7 us -> 11.4 us
  Pallas kernels: 27 us -> 26 us
  local copies, waits for them, and re-layouts: 0.03 us -> 0.9 us
    ppermute x3, waiting for transfers between devices: 0.57 us -> 7.66 us  [shift(): lax.ppermute(value, axis, [(s, (s + steps) % count) for s in range(count)])]
    ppermute x3, starting transfers between devices: 16.7 us -> 11.4 us  [shift(): lax.ppermute(value, axis, [(s, (s + steps) % count) for s in range(count)])]
    pallas_call x8 -> x9, Pallas kernels: 27 us -> 26 us  [call(): pl.pallas_call(body, out_shape=outs, scratch_shapes=scratch, compiler_par...]
    unnamed x10, local copies, waits for them, and re-layouts: 0.03 us -> 0.9 us
  transfers between devices with their start and end apart: 3 -> 3, of which waited for: 1 -> 2; matrix products, arithmetic and copies ran while one was open for 0% -> 0% of each run, Pallas kernels for 30% -> 10%
where the time goes in v5:
time: 46.2 us; the launch traced here: 46 us
  Pallas kernels  26 us (56%)
  starting transfers between devices  11.4 us (25%)
  waiting for transfers between devices  7.66 us (17%)
  local copies, waits for them, and re-layouts  0.9 us (2%)
    pallas_call x9, Pallas kernels, call(): pl.pallas_call(body, out_shape=outs, scratch_shapes=scratch, compiler_par...  26 us
    ppermute x3, starting transfers between devices, shift(): lax.ppermute(value, axis, [(s, (s + steps) % count) for s in range(count)])  11.4 us
    ppermute x3, waiting for transfers between devices, shift(): lax.ppermute(value, axis, [(s, (s + steps) % count) for s in range(count)])  7.66 us
  transfers between devices with their start and end apart: 3, of which 2 were waited for; matrix products, arithmetic and copies ran while one was open for 0% of the time, Pallas kernels for 10%

profile of v5, /device:TPU:1, one launch (start us, length us, event | category | flops | bytes accessed | tf_op | source)
XLA Modules:
  0.0 46.0 jit_solution(11532309382471129678)
XLA Ops:
  0.0 3.1 %shard_map.127 = (bf16[6,160,384]{2,1,0:T(8,128)(2,1)S(1)}, f32[8,512]{1,0:T(8,128)S(1)}, bf16[544,384]{1,0:T(8,128)(2,1)S(1)}, f32[13,16,256]{2,1,0:T(8,128)S(1...) custom-call(bf16[36,24,384]{2,1,0:T(8,128)(2,1)} %bitcast.4, ...), custom_call_target="tpu_custom_call" | custom-call | tf_op jit(solution)/shard_map/pallas_call | solution.py:405
  3.1 4.6 %shard_map.128 = (f32[3200,128]{1,0:T(8,128)S(1)}, f32[3200,128]{1,0:T(8,128)S(1)}, f32[3200,128]{1,0:T(8,128)S(1)}, f32[3200,128]{1,0:T(8,128)S(1)}, bf16[544,384]{1,0:T(8,128)(2,1)S(1)}) custom-call(f32[144,128]{1,0:T(8,128)S(1)} %get-tuple-element.34.refs_0_, f32[144,128]{1,0:T(8,128)S(1)} %get-tuple-element.35.refs_1_, ...), custom_call_target="tpu_custom_call", output_to_operand_aliasing={{4}: (7, {})} | custom-call | flops 3000000000 | bytes 8000000 | tf_op jit(solution)/shard_map/pallas_call | solution.py:405
  7.7 4.2 %collective-permute-start = (bf16[544,384]{1,0:T(8,128)(2,1)S(1)}, bf16[544,384]{1,0:T(8,128)(2,1)S(1)}, u32[]{:S(2)}, u32[]{:S(2)}) collective-permute-start(bf16[544,384]{1,0:T(8,128)(2,1)S(1)} %get-tuple-element.41), channel_id=1, source_target_pairs={{0,64},{64,0},{1,65},{65,1},{2,66},{66,2},{3,67},{67,3},{4,68},{68... | collective-permute-start | bytes 1253384 | tf_op jit(solution)/shard_map/ppermute | solution.py:420
  12.0 1.3 %collective-permute-done.lat.refs_6_ = bf16[544,384]{1,0:T(8,128)(2,1)S(1)} collective-permute-done((bf16[544,384]{1,0:T(8,128)(2,1)S(1)}, bf16[544,384]{1,0:T(8,128)(2,1)S(1)}, u32[]{:S(2)}, u32[]{:S(2)}) %collective-permute-start) | collective-permute-done | bytes 417824 | tf_op jit(solution)/shard_map/ppermute | solution.py:420
  13.3 4.6 %shard_map.131 = (f32[3200,128]{1,0:T(8,128)S(1)}, f32[3200,128]{1,0:T(8,128)S(1)}, f32[3200,128]{1,0:T(8,128)S(1)}, f32[3200,128]{1,0:T(8,128)S(1)}) custom-call(f32[144,128]{1,0:T(8,128)S(1)} %get-tuple-element.34.refs_0_, f32[144,128]{1,0:T(8,128)S(1)} %get-tuple-element.35.refs_1_, ...), custom_call_target="tpu_custom_call", output_to_operand_aliasing={{0}: (7, {}), {1}: (8, {}), {2}: (9, {}), {3}: (10, {})} | custom-call | flops 10000000000 | bytes 8000000 | tf_op jit(solution)/shard_map/pallas_call | solution.py:405
  18.0 5.2 %collective-permute-start.2 = (bf16[320,384]{1,0:T(8,128)(2,1)S(1)}, bf16[320,384]{1,0:T(8,128)(2,1)S(1)}, u32[]{:S(2)}, u32[]{:S(2)}) collective-permute-start(bf16[320,384]{1,0:T(8,128)(2,1)S(1)} %shard_map.132), channel_id=1, source_target_pairs={{0,63},{1,0},{2,1},{3,2},{4,3},{5,4},{6,5},{7,6},{8,7},{9,8},{10,9... | collective-permute-start | bytes 737288 | tf_op jit(solution)/shard_map/ppermute | solution.py:420
  23.2 1.9 %collective-permute-start.1 = (bf16[336,384]{1,0:T(8,128)(2,1)S(1)}, bf16[336,384]{1,0:T(8,128)(2,1)S(1)}, u32[]{:S(2)}, u32[]{:S(2)}) collective-permute-start(bf16[336,384]{1,0:T(8,128)(2,1)S(1)} %shard_map.129), channel_id=1, source_target_pairs={{0,1},{1,2},{2,3},{3,4},{4,5},{5,6},{6,7},{7,8},{8,9},{9,10},{10,1... | collective-permute-start | bytes 774152 | tf_op jit(solution)/shard_map/ppermute | solution.py:420
  25.2 0.0 copy-start.3
  25.2 0.3 shard_map.133
  25.5 0.9 %copy-done.3 = bf16[384,1152]{1,0:T(8,128)(2,1)S(1)} copy-done((bf16[384,1152]{1,0:T(8,128)(2,1)S(1)}, bf16[384,1152]{1,0:T(8,128)(2,1)}, u32[]{:S(2)}) %copy-start.3) | copy-done | bytes 884760
  26.3 0.0 copy-start
  26.3 0.0 copy-start.1
  26.4 0.0 copy-start.2
  26.4 0.0 copy-start.4
  26.4 4.1 %shard_map.134 = (f32[6,160,384]{2,1,0:T(8,128)S(1)}, f32[6,80,384]{2,1,0:T(8,128)S(1)}) custom-call(bf16[6,160,384]{2,1,0:T(8,128)(2,1)S(1)} %get-tuple-element.33.nq, bf16[544,384]{1,0:T(8,128)(2,1)S(1)} %collective-permute-done.lat.refs_6_, f32[8,512]{1,0:T(8,128)S(1)} %get-tuple-element.42.comb, f32[3200,128]{1,0:T(8,128)S(1)} %get-tuple-element.55.bm1, ...), custom_call_target="tpu_custom_call" | custom-call | flops 5000000000 | bytes 8000000 | tf_op jit(solution)/shard_map/pallas_call | solution.py:405
  30.5 0.0 collective-permute-done.2.right
  30.5 6.3 %collective-permute-done.1.left = bf16[336,384]{1,0:T(8,128)(2,1)S(1)} collective-permute-done((bf16[336,384]{1,0:T(8,128)(2,1)S(1)}, bf16[336,384]{1,0:T(8,128)(2,1)S(1)}, u32[]{:S(2)}, u32[]{:S(2)}) %collective-permute-start.1) | collective-permute-done | bytes 258080 | tf_op jit(solution)/shard_map/ppermute | solution.py:420
  36.8 0.0 copy-done
  36.8 0.0 copy-done.1
  36.9 0.0 copy-done.2
  36.9 0.0 copy-done.4
  36.9 9.1 %shard_map.135 = bf16[36,24,384]{2,1,0:T(8,128)(2,1)} custom-call(bf16[36,24,384]{2,1,0:T(8,128)(2,1)S(1)} %bitcast.5, bf16[6,160,384]{2,1,0:T(8,128)(2,1)S(1)} %get-tuple-element.33.nq, bf16[544,384]{1,0:T(8,128)(2,1)S(1)} %collective-permute-done.lat.refs_6_, bf16[336,384]{1,0:T(8,128)(2,1)S(1)} %collective-permute-done.1.left, ...), custom_call_target="tpu_custom_call" | custom-call | tf_op jit(solution)/shard_map/pallas_call | solution.py:405
  (3 shorter events, 0.1 us)
Async XLA Ops:
  7.7 5.6 %collective-permute-start = (bf16[544,384]{1,0:T(8,128)(2,1)S(1)}, bf16[544,384]{1,0:T(8,128)(2,1)S(1)}, u32[]{:S(2)}, u32[]{:S(2)}) collective-permute-start(bf16[544,384]{1,0:T(8,128)(2,1)S(1)} %get-tuple-element.41), channel_id=1, source_target_pairs={{0,64},{64,0},{1,65},{65,1},{2,66},{66,2},{3,67},{67,3},{4,68},{68... | collective-permute-start | bytes 1253384 | tf_op jit(solution)/shard_map/ppermute | solution.py:420
  18.0 12.5 %collective-permute-start.2 = (bf16[320,384]{1,0:T(8,128)(2,1)S(1)}, bf16[320,384]{1,0:T(8,128)(2,1)S(1)}, u32[]{:S(2)}, u32[]{:S(2)}) collective-permute-start(bf16[320,384]{1,0:T(8,128)(2,1)S(1)} %shard_map.132), channel_id=1, source_target_pairs={{0,63},{1,0},{2,1},{3,2},{4,3},{5,4},{6,5},{7,6},{8,7},{9,8},{10,9... | collective-permute-start | bytes 737288 | tf_op jit(solution)/shard_map/ppermute | solution.py:420
  23.2 13.6 %collective-permute-start.1 = (bf16[336,384]{1,0:T(8,128)(2,1)S(1)}, bf16[336,384]{1,0:T(8,128)(2,1)S(1)}, u32[]{:S(2)}, u32[]{:S(2)}) collective-permute-start(bf16[336,384]{1,0:T(8,128)(2,1)S(1)} %shard_map.129), channel_id=1, source_target_pairs={{0,1},{1,2},{2,3},{3,4},{4,5},{5,6},{6,7},{7,8},{8,9},{9,10},{10,1... | collective-permute-start | bytes 774152 | tf_op jit(solution)/shard_map/ppermute | solution.py:420
  25.2 1.2 %copy-start.3 = (bf16[384,1152]{1,0:T(8,128)(2,1)S(1)}, bf16[384,1152]{1,0:T(8,128)(2,1)}, u32[]{:S(2)}) copy-start(bf16[384,1152]{1,0:T(8,128)(2,1)} %w_qkv.3) | copy-start | bytes 2654212
  26.3 10.5 %copy-start = (bf16[2,18,24,384]{3,2,1,0:T(8,128)(2,1)S(1)}, bf16[2,18,24,384]{3,2,1,0:T(8,128)(2,1)}, u32[]{:S(2)}) copy-start(bf16[2,18,24,384]{3,2,1,0:T(8,128)(2,1)} %param.13) | copy-start | bytes 1990660
  26.3 10.5 %copy-start.1 = (bf16[384,1536]{1,0:T(8,128)(2,1)S(1)}, bf16[384,1536]{1,0:T(8,128)(2,1)}, u32[]{:S(2)}) copy-start(bf16[384,1536]{1,0:T(8,128)(2,1)} %w_fc1.1) | copy-start | bytes 3538948
  26.4 10.5 %copy-start.2 = (bf16[1536,384]{1,0:T(8,128)(2,1)S(1)}, bf16[1536,384]{1,0:T(8,128)(2,1)}, u32[]{:S(2)}) copy-start(bf16[1536,384]{1,0:T(8,128)(2,1)} %w_fc2.1) | copy-start | bytes 3538948
  26.4 10.5 %copy-start.4 = (bf16[384,384]{1,0:T(8,128)(2,1)S(1)}, bf16[384,384]{1,0:T(8,128)(2,1)}, u32[]{:S(2)}) copy-start(bf16[384,384]{1,0:T(8,128)(2,1)} %w_proj.1) | copy-start | bytes 884740

commit v6 on v5

--- a/solution.py
+++ b/solution.py
@@ -166,8 +166,9 @@
 def block_range(stage):
     lon = lax.axis_index("lon")
     first = jnp.where((lon == 0) & (lax.axis_index("lat") == 1) & (lax.axis_index("ens") == 0), 4, 0)
-    second = jnp.maximum(first, 2)
-    third = jnp.maximum(second, 8 - lon % 32)
+    second = jnp.where(lon % 32 == 31, 0, jnp.maximum(first, 2))
+    behind = (lon == 0) & (lax.axis_index("lat") == 0) & (lax.axis_index("ens") == 0)
+    third = jnp.where(behind, 4, jnp.maximum(second, 8 - lon % 32))
     return ((0, first), (first, second), (second, third), (third, 8))[stage]
 
 
@@ -443,15 +444,15 @@
         in_specs=[pl.BlockSpec(memory_space=pltpu.HBM)] * 9,
     )
 
-    def bias(stage, extra, kept):
-        count = len(kept)
+    def bias(stage, extra, kept, also=()):
+        count = len(kept) + len(also)
         table = (sds((ROWS * SPAN, 128), F32),) * 4
         alias = {7 + n: n for n in range(4)} if stage else {7: 4}
         return call(
             lambda *refs: bias_body(stage, *refs[:7], *refs[7 + count:]),
             table if stage else table + (sds(pay.shape, pay.dtype),),
             [vm((CHUNKS * ROWS, 256), F32)],
-            tuple(found) + (own, inner, extra) + kept,
+            tuple(found) + (own, inner, extra) + kept + also,
             in_specs=[pl.BlockSpec(memory_space=vm)] * 7 + [pl.BlockSpec(memory_space=vm if stage else pl.ANY)] * count,
             out_specs=tuple([pl.BlockSpec(memory_space=vm)] * 4 + [pl.BlockSpec(memory_space=pl.ANY)] * (not stage)),
             cost_estimate=pl.CostEstimate(flops=10 ** 10 if stage > 1 else 3 * 10 ** 9, transcendentals=0,
@@ -464,7 +465,7 @@
     some = bias(1, own, tuple(some))
     pay_r = call(right_body, sds((336, C), BF16), [pltpu.VMEM((320, C), F32)], (nq, lat, comb))
     left = shift(pay_r, "lon", 1)
-    some = bias(2, lat, tuple(some))
+    some = bias(2, lat, tuple(some), (w_qkv,))
     pay_l = call(
         left_body,
         sds((320, C), BF16),

time: 46.2 us -> 44.6 us (0.965)
  starting transfers between devices: 11.4 us -> 10.1 us
  local copies, waits for them, and re-layouts: 0.9 us -> 0.03 us
    ppermute x3, starting transfers between devices: 11.4 us -> 10.1 us  [shift(): lax.ppermute(value, axis, [(s, (s + steps) % count) for s in range(count)])]
    unnamed x10, local copies, waits for them, and re-layouts: 0.9 us -> 0.03 us
    ppermute x3, waiting for transfers between devices: 7.66 us -> 8.12 us  [shift(): lax.ppermute(value, axis, [(s, (s + steps) % count) for s in range(count)])]
where the time goes in v6:
time: 44.6 us; the launch traced here: 44.4 us
  Pallas kernels  26 us (58%)
  starting transfers between devices  10.1 us (23%)
  waiting for transfers between devices  8.12 us (18%)
    pallas_call x9, Pallas kernels, call(): pl.pallas_call(body, out_shape=outs, scratch_shapes=scratch, compiler_par...  26 us
    ppermute x3, starting transfers between devices, shift(): lax.ppermute(value, axis, [(s, (s + steps) % count) for s in range(count)])  10.1 us
    ppermute x3, waiting for transfers between devices, shift(): lax.ppermute(value, axis, [(s, (s + steps) % count) for s in range(count)])  8.12 us
  transfers between devices with their start and end apart: 3, of which 2 were waited for; matrix products, arithmetic and copies ran while one was open for 0% of the time, Pallas kernels for 10%

profile of v6, /device:TPU:1, one launch (start us, length us, event | category | flops | bytes accessed | tf_op | source)
XLA Modules:
  0.0 44.4 jit_solution(3568745461829140563)
XLA Ops:
  0.0 3.1 %shard_map.127 = (bf16[6,160,384]{2,1,0:T(8,128)(2,1)S(1)}, f32[8,512]{1,0:T(8,128)S(1)}, bf16[544,384]{1,0:T(8,128)(2,1)S(1)}, f32[13,16,256]{2,1,0:T(8,128)S(1...) custom-call(bf16[36,24,384]{2,1,0:T(8,128)(2,1)} %bitcast.4, ...), custom_call_target="tpu_custom_call" | custom-call | tf_op jit(solution)/shard_map/pallas_call | solution.py:406
  3.1 4.6 %shard_map.128 = (f32[3200,128]{1,0:T(8,128)S(1)}, f32[3200,128]{1,0:T(8,128)S(1)}, f32[3200,128]{1,0:T(8,128)S(1)}, f32[3200,128]{1,0:T(8,128)S(1)}, bf16[544,384]{1,0:T(8,128)(2,1)S(1)}) custom-call(f32[144,128]{1,0:T(8,128)S(1)} %get-tuple-element.34.refs_0_, f32[144,128]{1,0:T(8,128)S(1)} %get-tuple-element.35.refs_1_, ...), custom_call_target="tpu_custom_call", output_to_operand_aliasing={{4}: (7, {})} | custom-call | flops 3000000000 | bytes 8000000 | tf_op jit(solution)/shard_map/pallas_call | solution.py:406
  7.7 4.2 %collective-permute-start = (bf16[544,384]{1,0:T(8,128)(2,1)S(1)}, bf16[544,384]{1,0:T(8,128)(2,1)S(1)}, u32[]{:S(2)}, u32[]{:S(2)}) collective-permute-start(bf16[544,384]{1,0:T(8,128)(2,1)S(1)} %get-tuple-element.41), channel_id=1, source_target_pairs={{0,64},{64,0},{1,65},{65,1},{2,66},{66,2},{3,67},{67,3},{4,68},{68... | collective-permute-start | bytes 1253384 | tf_op jit(solution)/shard_map/ppermute | solution.py:421
  12.0 0.0 copy-start.3
  12.0 1.3 %collective-permute-done.lat.refs_6_ = bf16[544,384]{1,0:T(8,128)(2,1)S(1)} collective-permute-done((bf16[544,384]{1,0:T(8,128)(2,1)S(1)}, bf16[544,384]{1,0:T(8,128)(2,1)S(1)}, u32[]{:S(2)}, u32[]{:S(2)}) %collective-permute-start) | collective-permute-done | bytes 417824 | tf_op jit(solution)/shard_map/ppermute | solution.py:421
  13.3 0.0 copy-done.3
  13.3 4.6 %shard_map.131 = (f32[3200,128]{1,0:T(8,128)S(1)}, f32[3200,128]{1,0:T(8,128)S(1)}, f32[3200,128]{1,0:T(8,128)S(1)}, f32[3200,128]{1,0:T(8,128)S(1)}) custom-call(f32[144,128]{1,0:T(8,128)S(1)} %get-tuple-element.34.refs_0_, f32[144,128]{1,0:T(8,128)S(1)} %get-tuple-element.35.refs_1_, ...), custom_call_target="tpu_custom_call", output_to_operand_aliasing={{0}: (7, {}), {1}: (8, {}), {2}: (9, {}), {3}: (10, {})} | custom-call | flops 10000000000 | bytes 8000000 | tf_op jit(solution)/shard_map/pallas_call | solution.py:406
  18.0 4.0 %collective-permute-start.2 = (bf16[320,384]{1,0:T(8,128)(2,1)S(1)}, bf16[320,384]{1,0:T(8,128)(2,1)S(1)}, u32[]{:S(2)}, u32[]{:S(2)}) collective-permute-start(bf16[320,384]{1,0:T(8,128)(2,1)S(1)} %shard_map.132), channel_id=1, source_target_pairs={{0,63},{1,0},{2,1},{3,2},{4,3},{5,4},{6,5},{7,6},{8,7},{9,8},{10,9... | collective-permute-start | bytes 737288 | tf_op jit(solution)/shard_map/ppermute | solution.py:421
  22.0 1.9 %collective-permute-start.1 = (bf16[336,384]{1,0:T(8,128)(2,1)S(1)}, bf16[336,384]{1,0:T(8,128)(2,1)S(1)}, u32[]{:S(2)}, u32[]{:S(2)}) collective-permute-start(bf16[336,384]{1,0:T(8,128)(2,1)S(1)} %shard_map.129), channel_id=1, source_target_pairs={{0,1},{1,2},{2,3},{3,4},{4,5},{5,6},{6,7},{7,8},{8,9},{9,10},{10,1... | collective-permute-start | bytes 774152 | tf_op jit(solution)/shard_map/ppermute | solution.py:421
  23.9 0.3 shard_map.133
  24.2 0.0 copy-start
  24.2 0.0 copy-start.1
  24.3 0.0 copy-start.2
  24.3 0.0 copy-start.4
  24.3 4.1 %shard_map.134 = (f32[6,160,384]{2,1,0:T(8,128)S(1)}, f32[6,80,384]{2,1,0:T(8,128)S(1)}) custom-call(bf16[6,160,384]{2,1,0:T(8,128)(2,1)S(1)} %get-tuple-element.33.nq, bf16[544,384]{1,0:T(8,128)(2,1)S(1)} %collective-permute-done.lat.refs_6_, f32[8,512]{1,0:T(8,128)S(1)} %get-tuple-element.42.comb, f32[3200,128]{1,0:T(8,128)S(1)} %get-tuple-element.55.bm1, ...), custom_call_target="tpu_custom_call" | custom-call | flops 5000000000 | bytes 8000000 | tf_op jit(solution)/shard_map/pallas_call | solution.py:406
  28.4 0.0 collective-permute-done.2.right
  28.4 6.8 %collective-permute-done.1.left = bf16[336,384]{1,0:T(8,128)(2,1)S(1)} collective-permute-done((bf16[336,384]{1,0:T(8,128)(2,1)S(1)}, bf16[336,384]{1,0:T(8,128)(2,1)S(1)}, u32[]{:S(2)}, u32[]{:S(2)}) %collective-permute-start.1) | collective-permute-done | bytes 258080 | tf_op jit(solution)/shard_map/ppermute | solution.py:421
  35.3 0.0 copy-done
  35.3 0.0 copy-done.1
  35.3 0.0 copy-done.2
  35.3 0.0 copy-done.4
  35.3 9.1 %shard_map.135 = bf16[36,24,384]{2,1,0:T(8,128)(2,1)} custom-call(bf16[36,24,384]{2,1,0:T(8,128)(2,1)S(1)} %bitcast.5, bf16[6,160,384]{2,1,0:T(8,128)(2,1)S(1)} %get-tuple-element.33.nq, bf16[544,384]{1,0:T(8,128)(2,1)S(1)} %collective-permute-done.lat.refs_6_, bf16[336,384]{1,0:T(8,128)(2,1)S(1)} %collective-permute-done.1.left, ...), custom_call_target="tpu_custom_call" | custom-call | tf_op jit(solution)/shard_map/pallas_call | solution.py:406
  (3 shorter events, 0.1 us)
Async XLA Ops:
  7.7 5.6 %collective-permute-start = (bf16[544,384]{1,0:T(8,128)(2,1)S(1)}, bf16[544,384]{1,0:T(8,128)(2,1)S(1)}, u32[]{:S(2)}, u32[]{:S(2)}) collective-permute-start(bf16[544,384]{1,0:T(8,128)(2,1)S(1)} %get-tuple-element.41), channel_id=1, source_target_pairs={{0,64},{64,0},{1,65},{65,1},{2,66},{66,2},{3,67},{67,3},{4,68},{68... | collective-permute-start | bytes 1253384 | tf_op jit(solution)/shard_map/ppermute | solution.py:421
  12.0 1.4 %copy-start.3 = (bf16[384,1152]{1,0:T(8,128)(2,1)S(1)}, bf16[384,1152]{1,0:T(8,128)(2,1)}, u32[]{:S(2)}) copy-start(bf16[384,1152]{1,0:T(8,128)(2,1)} %w_qkv.3) | copy-start | bytes 2654212
  18.0 10.4 %collective-permute-start.2 = (bf16[320,384]{1,0:T(8,128)(2,1)S(1)}, bf16[320,384]{1,0:T(8,128)(2,1)S(1)}, u32[]{:S(2)}, u32[]{:S(2)}) collective-permute-start(bf16[320,384]{1,0:T(8,128)(2,1)S(1)} %shard_map.132), channel_id=1, source_target_pairs={{0,63},{1,0},{2,1},{3,2},{4,3},{5,4},{6,5},{7,6},{8,7},{9,8},{10,9... | collective-permute-start | bytes 737288 | tf_op jit(solution)/shard_map/ppermute | solution.py:421
  22.0 13.2 %collective-permute-start.1 = (bf16[336,384]{1,0:T(8,128)(2,1)S(1)}, bf16[336,384]{1,0:T(8,128)(2,1)S(1)}, u32[]{:S(2)}, u32[]{:S(2)}) collective-permute-start(bf16[336,384]{1,0:T(8,128)(2,1)S(1)} %shard_map.129), channel_id=1, source_target_pairs={{0,1},{1,2},{2,3},{3,4},{4,5},{5,6},{6,7},{7,8},{8,9},{9,10},{10,1... | collective-permute-start | bytes 774152 | tf_op jit(solution)/shard_map/ppermute | solution.py:421
  24.2 11.0 %copy-start = (bf16[2,18,24,384]{3,2,1,0:T(8,128)(2,1)S(1)}, bf16[2,18,24,384]{3,2,1,0:T(8,128)(2,1)}, u32[]{:S(2)}) copy-start(bf16[2,18,24,384]{3,2,1,0:T(8,128)(2,1)} %param.13) | copy-start | bytes 1990660
  24.2 11.0 %copy-start.1 = (bf16[384,1536]{1,0:T(8,128)(2,1)S(1)}, bf16[384,1536]{1,0:T(8,128)(2,1)}, u32[]{:S(2)}) copy-start(bf16[384,1536]{1,0:T(8,128)(2,1)} %w_fc1.1) | copy-start | bytes 3538948
  24.3 11.0 %copy-start.2 = (bf16[1536,384]{1,0:T(8,128)(2,1)S(1)}, bf16[1536,384]{1,0:T(8,128)(2,1)}, u32[]{:S(2)}) copy-start(bf16[1536,384]{1,0:T(8,128)(2,1)} %w_fc2.1) | copy-start | bytes 3538948
  24.3 11.0 %copy-start.4 = (bf16[384,384]{1,0:T(8,128)(2,1)S(1)}, bf16[384,384]{1,0:T(8,128)(2,1)}, u32[]{:S(2)}) copy-start(bf16[384,384]{1,0:T(8,128)(2,1)} %w_proj.1) | copy-start | bytes 884740
